TPU v7x, 128 devices: a whole 4x4x4 slice. The times are simulated.
128 devices in a mesh: sa: 8 (over x, core), an: 16 (over y, z).
Axes of the slice: x: 4, y: 4, z: 4, core: 2. Of those that a mesh axis runs over, the one named last changes fastest.
Arguments:
- decoder_states: bfloat16 [8192, 4096], P('sa', 'an'), may hold values from -170 to 170
- w_query: bfloat16 [4096, 4096], P(None, 'an'), may hold values from -0.09375 to 0.09375
- w_key: bfloat16 [1024, 4096], P(None, 'an'), may hold values from -0.1875 to 0.1875
- w_value: bfloat16 [1024, 4096], P(None, 'an'), may hold values from -0.1875 to 0.1875
- w_out: bfloat16 [4096, 4096], P('an'), may hold values from -0.375 to 0.375
- enc_up: bfloat16 [1024, 4096], replicated, may hold values from -0.1875 to 0.1875
- enc_down: bfloat16 [4096, 1024], replicated, may hold values from -0.09375 to 0.09375
- neighbour_inputs: bfloat16 [1024, 128, 1024], P(('sa', 'an')), may hold values from -6 to 6
- requests: int32 [256], P('sa'), may hold values from 0 to 127, as said below
Outputs:
- cross_output: bfloat16 [8192, 4096], P('sa', 'an')
Inputs may be any that keep to these rules, and one draw needn't show every extreme that they name: Within each block of 32 requests (one index of sa) the owner of a request is its value // 8; no owner receives more than 4 requests of a block and no more than 2 distinct neighbours of one owner are requested in a block; in every block some owner receives exactly 4 requests, 2 of them distinct. A neighbour may be requested several times.
All inputs are finite; a program needn't handle non-finite values.
Results may differ from a plain program's by a relative error of at most 0.01.
The roundings to bfloat16 on the way count: a program that leaves them out, or rounds other values in their place, can miss the bound.
Values may be sent and summed in bfloat16 or wider, within the bound.
A program may use at most 128 MiB of HBM per device.

v0:
```python
import jax
import jax.numpy as jnp
from jax import lax
from jax.sharding import PartitionSpec as P

D = 4096
HEADS = 32
GROUP = 64
NEIGH = 2


EPS = 1e-06


def encode(rows, enc_up, enc_down):
    wide = rows.astype(jnp.float32)
    square = jnp.mean(wide * wide, axis=-1, keepdims=True)
    normed = (wide * lax.rsqrt(square + EPS)).astype(jnp.bfloat16)
    hidden = jax.nn.gelu(
        jnp.dot(normed, enc_up, preferred_element_type=jnp.float32), approximate=False
    ).astype(jnp.bfloat16)
    return (wide + jnp.dot(hidden, enc_down, preferred_element_type=jnp.float32)).astype(
        jnp.bfloat16
    )


def shards(
    decoder_states, w_query, w_key, w_value, w_out, enc_up, enc_down, neighbour_inputs, requests
):
    owner_total = lax.axis_size("an")
    position = lax.axis_index("an")
    tok_rows, local_width = decoder_states.shape
    head_dim = D // HEADS
    heads_here = local_width // head_dim
    scale = float(head_dim) ** (-0.5)
    total_requests = requests.shape[0]
    per_owner = total_requests // owner_total
    nb_own = neighbour_inputs.shape[0]
    span = neighbour_inputs.shape[1]
    owner = requests // nb_own
    local_id = requests % nb_own
    owner_range = jnp.arange(owner_total, dtype=jnp.int32)
    local_range = jnp.arange(nb_own, dtype=jnp.int32)
    hits = (owner[:, None, None] == owner_range[None, :, None]) & (
        local_id[:, None, None] == local_range[None, None, :]
    )
    present = jnp.any(hits, axis=0).astype(jnp.int32)
    ranked = jnp.cumsum(present, axis=1) - present
    slot_of_request = owner * per_owner + ranked[owner, local_id]
    my_present = jnp.sum(jnp.where(owner_range[:, None] == position, present, 0), axis=0)
    my_rank = jnp.sum(jnp.where(owner_range[:, None] == position, ranked, 0), axis=0)
    chosen_mask = (my_present[:, None] == 1) & (
        my_rank[:, None] == jnp.arange(per_owner, dtype=jnp.int32)[None, :]
    )
    local_of_slot = jnp.sum(jnp.where(chosen_mask, local_range[:, None], 0), axis=0)
    rows = w_query
    queries = jnp.dot(
        lax.all_gather(decoder_states, "an", axis=1, tiled=True),
        rows,
        preferred_element_type=jnp.float32,
    )
    chosen = neighbour_inputs[local_of_slot].reshape(per_owner * span, neighbour_inputs.shape[2])
    encoded = encode(chosen, enc_up, enc_down)
    both_weights = jnp.concatenate([w_key, w_value], axis=1)
    projected = jnp.dot(
        lax.all_gather(encoded, "an", axis=0, tiled=True),
        both_weights,
        preferred_element_type=jnp.float32,
    ).astype(jnp.bfloat16)
    projected = projected.reshape(owner_total * per_owner, span, 2 * local_width)
    groups = tok_rows // GROUP
    selected = projected[slot_of_request].reshape(groups, NEIGH * span, 2 * local_width)
    keys = selected[:, :, :local_width].reshape(groups, NEIGH * span, heads_here, head_dim)
    values = selected[:, :, local_width:].reshape(groups, NEIGH * span, heads_here, head_dim)
    queries = queries.astype(jnp.bfloat16).reshape(groups, GROUP, heads_here, head_dim)
    scores = (
        jnp.einsum("cqhd,ckhd->chqk", queries, keys, preferred_element_type=jnp.float32) * scale
    )
    top = jnp.max(scores, axis=-1, keepdims=True)
    weights = jnp.exp(scores - top)
    probs = (weights / jnp.sum(weights, axis=-1, keepdims=True)).astype(jnp.bfloat16)
    attended = jnp.einsum(
        "chqk,ckhd->cqhd", probs, values, preferred_element_type=jnp.float32
    ).astype(jnp.bfloat16)
    attended = attended.reshape(tok_rows, local_width)
    column_block = lax.all_to_all(w_out, "an", split_axis=1, concat_axis=0, tiled=True)
    rows = column_block
    summed = jnp.dot(
        lax.all_gather(attended, "an", axis=1, tiled=True), rows, preferred_element_type=jnp.float32
    )
    return summed.astype(jnp.bfloat16)


def solution(mesh):
    placed = (
        P("sa", "an"),
        P(None, "an"),
        P(None, "an"),
        P(None, "an"),
        P("an", None),
        P(),
        P(),
        P(("sa", "an"), None, None),
        P("sa"),
    )
    return jax.shard_map(
        shards, mesh=mesh, in_specs=placed, out_specs=P("sa", "an"), check_vma=False
    )
```

profile of v0, /device:TPU:1, one launch (start us, length us, event | category | flops | bytes accessed | tf_op | source)
XLA Modules:
  0.0 301.0 jit_solution(9796901206107320811)
XLA Ops:
  6.5 0.8 fusion.66
  7.4 0.4 and_reduce_fusion
  7.8 0.2 reduce_window_sum.11
  7.9 0.1 select_reduce_fusion
  8.0 0.1 fusion.62
  8.2 0.6 gather_fusion
  8.8 0.2 multiply_reduce_fusion.1
  9.0 0.2 fusion.54
  9.2 17.1 %fusion.47 = bf16[256,1024]{1,0:T(8,128)(2,1)} fusion(bf16[4096,1024]{1,0:T(8,128)(2,1)} %param.15, bf16[256,1024]{1,0:T(8,128)(2,1)S(1)} %fusion.54, bf16[1024,4096]{1,0:T(8,128)(2,1)} %param.14, bf16[256,1024]{1,0:T(8,128)(2,1)S(1)} %bitcast.39), kind=kOutput, calls=%fused_computation.63 | convolution fusion | flops 4363911168 | bytes 18350080 | tf_op jit(solution)/shard_map/dot_general | solution.py:22
  26.3 0.7 all-gather.6.cloned.1.call-update
  27.0 0.2 all-gather.8.cloned.1.call-start
  27.3 0.7 gather_fusion.1
  28.0 72.4 %all-gather.4.cloned.1.call-done = bf16[4096,1024]{1,0:T(8,128)(2,1)} async-done(((bf16[256,1024]{1,0:T(8,128)(2,1)}), bf16[4096,1024]{1,0:T(8,128)(2,1)}) %all-gather.4.cloned.1.call-update) | async-done | bytes 8388624 | tf_op jit(solution)/shard_map/all_gather | solution.py:66
  100.4 9.6 %convolution_convert_fusion = bf16[4096,512]{1,0:T(8,128)(2,1)} fusion(bf16[4096,1024]{1,0:T(8,128)(2,1)} %all-gather.4.cloned.1.call-done, bf16[1024,256]{1,0:T(8,128)(2,1)S(1)} %copy-done.4, bf16[1024,256]{1,0:T(8,128)(2,1)S(1)} %copy-done.5), kind=kOutput, calls=%fused_computation.5 | convolution fusion | flops 4299161600 | bytes 13631488 | tf_op jit(solution)/shard_map/dot_general | solution.py:65
  110.0 5.1 %gather_fusion.2 = bf16[32,128,512]{2,1,0:T(8,128)(2,1)} fusion(bf16[32,128,512]{2,1,0:T(8,128)(2,1)} %bitcast.40, s32[1024]{0:T(1024)S(1)} %pad_clamp_fusion), kind=kCustom, calls=%fused_computation.2 | custom fusion | bytes 8388736 | tf_op jit(solution)/shard_map/gather | solution.py:72
  115.1 4.0 %fusion.104 = (bf16[16,256,256]{2,1,0:T(8,128)(2,1)}, bf16[16,256,256]{2,1,0:T(8,128)(2,1)S(1)}) fusion(bf16[16,256,512]{2,1,0:T(8,128)(2,1)} %bitcast.35), kind=kLoop, calls=%fused_computation.137 | loop fusion | bytes 8388608 | tf_op jit(solution)/shard_map/slice | solution.py:73
  119.1 2.4 copy.23
  121.5 2.8 copy.24
  124.4 53.9 %all-gather.6.cloned.1.call-done = bf16[1024,4096]{1,0:T(8,128)(2,1)} async-done(((bf16[1024,256]{1,0:T(8,128)(2,1)}), bf16[1024,4096]{1,0:T(8,128)(2,1)}) %all-gather.6.cloned.1.call-update) | async-done | bytes 8388624 | tf_op jit(solution)/shard_map/all_gather | solution.py:58
  178.3 6.3 %convolution_convert_fusion.3 = bf16[1024,256]{1,0:T(8,128)(2,1)S(1)} fusion(bf16[1024,4096]{1,0:T(8,128)(2,1)} %all-gather.6.cloned.1.call-done, bf16[4096,256]{1,0:T(8,128)(2,1)} %param.10), kind=kOutput, calls=%fused_computation.62 | convolution fusion | flops 2147745792 | bytes 11010048 | tf_op jit(solution)/shard_map/dot_general | solution.py:57
  184.6 0.1 reshape.115
  184.7 0.4 fusion.56
  185.2 0.8 fusion.105
  185.9 0.6 copy-done.3
  186.5 6.0 %fusion.50 = bf16[16,64,2,128]{3,1,2,0:T(8,128)(2,1)S(1)} fusion(bf16[16,256,2,128]{1,3,2,0:T(8,128)(2,1)} %bitcast.41, f32[16,2,64]{2,1,0:T(2,128)S(1)} %fusion.105, f32[16,2,64,256]{3,2,1,0:T(8,128)} %copy-done.3), kind=kOutput, calls=%fused_computation.64 | convolution fusion | flops 136579328 | bytes 4726784 | tf_op jit(solution)/shard_map/chqk,ckhd->cqhd/dot_general | solution.py:82
  192.5 0.6 copy.28
  193.1 0.9 copy.37
  194.0 2.5 copy.29
  196.5 37.9 %all_to_all.19 = bf16[256,16,256]{0,2,1:T(8,128)(2,1)S(1)} all-to-all(bf16[256,16,256]{0,2,1:T(8,128)(2,1)} %bitcast.38), channel_id=1, replica_groups=mesh['sa'=8,'an'=16] {'an'}, dimensions={1} | all-to-all | bytes 4194304 | tf_op jit(solution)/shard_map/all_to_all | solution.py:86
  234.4 2.4 copy.30
  236.9 50.3 %all-gather.8.cloned.1.call-done = bf16[1024,4096]{1,0:T(8,128)(2,1)} async-done(((bf16[1024,256]{1,0:T(8,128)(2,1)}), bf16[1024,4096]{1,0:T(8,128)(2,1)}) %all-gather.8.cloned.1.call-update) | async-done | bytes 8388624 | tf_op jit(solution)/shard_map/all_gather | solution.py:89
  287.2 7.2 %convolution_convert_fusion.1 = bf16[1024,256]{1,0:T(8,128)(2,1)} fusion(bf16[1024,4096]{1,0:T(8,128)(2,1)} %all-gather.8.cloned.1.call-done, bf16[4096,256]{1,0:T(8,128)(2,1)} %bitcast.42), kind=kOutput, calls=%fused_computation.60 | convolution fusion | flops 2147745792 | bytes 11010048 | tf_op jit(solution)/shard_map/dot_general | solution.py:88
  (25 shorter events, 0.2 us)
Async XLA Ops:
  6.5 1.6 copy-start
  6.5 93.9 %all-gather.4.cloned.1.call-start = ((), (), s32[]{:S(2)}) async-start(), calls=%async_computation.1 | async-start | bytes 8912896 | tf_op jit(solution)/shard_map/all_gather | solution.py:66
  9.1 91.3 %copy-start.4 = (bf16[1024,256]{1,0:T(8,128)(2,1)S(1)}, bf16[1024,256]{1,0:T(8,128)(2,1)}, u32[]{:S(2)}) copy-start(bf16[1024,256]{1,0:T(8,128)(2,1)} %param.12) | copy-start | bytes 1572868
  9.1 91.3 %copy-start.5 = (bf16[1024,256]{1,0:T(8,128)(2,1)S(1)}, bf16[1024,256]{1,0:T(8,128)(2,1)}, u32[]{:S(2)}) copy-start(bf16[1024,256]{1,0:T(8,128)(2,1)} %param.11) | copy-start | bytes 1572868
  26.3 152.0 %all-gather.6.cloned.1.call-start = ((), (), s32[]{:S(2)}) async-start(), calls=%async_computation.2 | async-start | bytes 8912896 | tf_op jit(solution)/shard_map/all_gather | solution.py:58
  27.0 260.2 %all-gather.8.cloned.1.call-start = ((), (), s32[]{:S(2)}) async-start(), calls=%async_computation.3 | async-start | bytes 8912896 | tf_op jit(solution)/shard_map/all_gather | solution.py:89
  185.2 1.4 copy-start.3
  186.5 7.5 %copy-start.2 = (bf16[256,4096]{1,0:T(8,128)(2,1)S(1)}, bf16[256,4096]{1,0:T(8,128)(2,1)}, u32[]{:S(2)}) copy-start(bf16[256,4096]{1,0:T(8,128)(2,1)} %param.13) | copy-start | bytes 6291460
  287.2 7.3 %copy-start.1 = (bf16[8,128,1024]{2,1,0:T(8,128)(2,1)S(1)}, bf16[8,128,1024]{2,1,0:T(8,128)(2,1)}, u32[]{:S(2)}) copy-start(bf16[8,128,1024]{2,1,0:T(8,128)(2,1)} %param.16) | copy-start | bytes 6291460
Sparse Core Ops, SparseCore 0:
  26.4 73.9 all-gather.3
  102.5 75.7 all-gather.5
  194.1 93.0 all-gather.7
where the time goes:
time: 302 us; the launch traced here: 301 us
  waiting for transfers between devices  177 us (59%)
  matrix products  46.7 us (15%)
  blocking collectives  37.9 us (13%)
  local copies, waits for them, and re-layouts  22.8 us (8%)
  between operations  13.2 us (4%)
    all_gather x1, waiting for transfers between devices, shards(): lax.all_gather(encoded, 'an', axis=0, tiled=True)  72.4 us
    all_gather x1, waiting for transfers between devices, shards(): lax.all_gather(decoder_states, 'an', axis=1, tiled=True)  53.9 us
    all_gather x1, waiting for transfers between devices, shards(): lax.all_gather(attended, 'an', axis=1, tiled=True)  50.3 us
    all_to_all x1, blocking collectives, shards(): lax.all_to_all(w_out, 'an', split_axis=1, concat_axis=0, tiled=True)  37.9 us
    dot_general x1, matrix products, encode(): jnp.dot(hidden, enc_down, preferred_element_type=jnp.float32)  17.1 us
    dot_general x1, matrix products, shards(): jnp.dot(lax.all_gather(encoded, 'an', axis=0, tiled=True), both_weights,...  9.6 us
    dot_general x1, matrix products, shards(): jnp.dot(lax.all_gather(attended, 'an', axis=1, tiled=True), rows, preferr...  7.25 us
    slice x2, local copies, waits for them, and re-layouts, shards(): selected[:, :, :local_width]  6.87 us
  transfers between devices with their start and end apart: 3, of which 3 were waited for; matrix products, arithmetic and copies ran while one was open for 10% of the time, Pallas kernels for 0%

commit v1 on v0

v1 whole, which is shorter than its diff:
```python
import functools

import jax
import jax.numpy as jnp
from jax import lax
from jax.experimental import pallas as pl
from jax.experimental.pallas import tpu as pltpu
from jax.sharding import PartitionSpec as P

HEAD = 128
GROUP = 64
NEIGH = 2
EPS = 1e-06
SIDE = 4
PLANE = SIDE * SIDE
LINE = 8
FCHUNK = 512
MESSAGES = 20
F32 = jnp.float32
BF16 = jnp.bfloat16


class Gather:
    def __init__(self, number, buf, send, recv, row, y, z):
        self.number, self.buf, self.send, self.recv = number, buf, send, recv
        self.row, self.y, self.z = row, y, z
        self.half = buf.shape[1] // 2

    def block(self, h, dp, dq):
        dy = dp * (1 - h) + dq * h
        dz = dq * (1 - h) + dp * h
        return ((self.y + dy) % SIDE) * SIDE + (self.z + dz) % SIDE

    def copy(self, h, msg, dp, dq, part, to):
        rows = self.half
        first = h * rows
        if part is not None:
            rows = rows // 2
            first += part * rows
        ref = self.buf.at[self.block(h, dp, dq), pl.ds(first, rows)]
        k = h * MESSAGES + msg
        return pltpu.make_async_remote_copy(
            src_ref=ref,
            dst_ref=ref,
            send_sem=self.send.at[self.number, k],
            recv_sem=self.recv.at[self.number, k],
            device_id={"sa": self.row, "an": self.block(h, *to)},
            device_id_type=pl.DeviceIdType.MESH,
        )

    def first_ring(self, h):
        self.copy(h, 0, 0, 0, None, (1, 0)).start()
        self.copy(h, 1, 0, 0, None, (3, 0)).start()

    def second_ring(self, h, i):
        self.copy(h, 4 + i, i, 0, None, (0, 1)).start()
        self.copy(h, 8 + i, i, 0, None, (0, 3)).start()

    def wait(self, h, msg, dp, dq, part):
        self.copy(h, msg, dp, dq, part, (1, 0)).wait_recv()

    def event1(self):
        for h in (0, 1):
            self.wait(h, 0, 3, 0, None)
            self.copy(h, 2, 3, 0, 0, (1, 0)).start()
            self.second_ring(h, 3)
        for h in (0, 1):
            self.wait(h, 1, 1, 0, None)
            self.copy(h, 3, 1, 0, 1, (3, 0)).start()
            self.second_ring(h, 1)

    def pass_on(self, h, i):
        self.wait(h, 4 + i, i, 3, None)
        self.copy(h, 12 + i, i, 3, 0, (0, 1)).start()
        self.wait(h, 8 + i, i, 1, None)
        self.copy(h, 16 + i, i, 1, 1, (0, 3)).start()

    def event2(self):
        for h in (0, 1):
            self.pass_on(h, 0)

    def event3(self):
        for h in (0, 1):
            self.wait(h, 2, 2, 0, 0)
            self.wait(h, 3, 2, 0, 1)
            self.second_ring(h, 2)

    def event4(self):
        for i in (3, 1):
            for h in (0, 1):
                self.pass_on(h, i)

    def event5(self):
        for h in (0, 1):
            self.pass_on(h, 2)

    def event6(self):
        for i in (0, 3, 1, 2):
            for h in (0, 1):
                self.wait(h, 12 + i, i, 2, 0)
                self.wait(h, 16 + i, i, 2, 1)

    def sent(self):
        for h in (0, 1):
            for msg in range(MESSAGES):
                part = None if msg < 2 or 4 <= msg < 12 else 0
                self.copy(h, msg, 0, 0, part, (1, 0)).wait_send()


ARRIVED = {
    0: (2, lambda i: (i, 0, 0)),
    1: (4, lambda i: (i // 2, 1 + 2 * (i % 2), 0)),
    2: (4, lambda i: (i // 2, 0, 1 + 2 * (i % 2))),
    3: (2, lambda i: (i, 2, 0)),
    4: (8, lambda i: (i // 4, 1 + 2 * ((i // 2) % 2), 1 + 2 * (i % 2))),
    5: (4, lambda i: (i // 2, 2, 1 + 2 * (i % 2))),
    6: (8, lambda i: (i // 4, i % 4, 2)),
}


def body(
    table, states, w_query, w_key, w_value, w_out, enc_up, enc_down, nearby, out,
    sgat, egat, agat, wcol, wq, wkv, wrow, up, down, pool,
    wide, normed, qs, keys, vals, total,
    send, recv, wsend, wrecv, lsend, lrecv, local, wsem,
):
    row = lax.axis_index("sa")
    me = lax.axis_index("an")
    y, z = me // SIDE, me % SIDE
    tokens, width = states.shape
    wrows = w_out.shape[0] // LINE
    chunks = enc_up.shape[1] // FCHUNK

    loads = [
        pltpu.make_async_copy(states, sgat.at[me], local.at[0]),
        pltpu.make_async_copy(w_out.at[pl.ds(row * wrows, wrows)], wrow, local.at[1]),
        pltpu.make_async_copy(nearby, pool, local.at[2]),
        pltpu.make_async_copy(w_query, wq, local.at[3]),
        pltpu.make_async_copy(w_key, wkv.at[:, pl.ds(0, width)], local.at[4]),
        pltpu.make_async_copy(w_value, wkv.at[:, pl.ds(width, width)], local.at[5]),
        pltpu.make_async_copy(
            w_out.at[pl.ds(row * wrows, wrows), pl.ds(me * width, width)],
            wcol.at[me, row],
            local.at[6],
        ),
    ]

    def load_up(f):
        cut = pl.ds(f * FCHUNK, FCHUNK)
        return pltpu.make_async_copy(enc_up.at[:, cut], up.at[:, cut], wsem.at[0, f])

    def load_down(f):
        cut = pl.ds(f * FCHUNK, FCHUNK)
        return pltpu.make_async_copy(enc_down.at[cut], down.at[cut], wsem.at[1, f])

    for i in (0, 2, 1, 6):
        loads[i].start()
    for f in range(chunks):
        load_up(f).start()
        load_down(f).start()
    for i in (4, 5, 3):
        loads[i].start()

    barrier = pltpu.get_barrier_semaphore()

    def greet_plane(k, carry):
        pl.semaphore_signal(
            barrier, inc=1, device_id={"sa": row, "an": (me + k) % PLANE},
            device_id_type=pl.DeviceIdType.MESH,
        )
        return carry

    def greet_line(k, carry):
        pl.semaphore_signal(
            barrier, inc=1, device_id={"sa": (row + k) % LINE, "an": me},
            device_id_type=pl.DeviceIdType.MESH,
        )
        return carry

    lax.fori_loop(1, PLANE, greet_plane, 0)
    lax.fori_loop(1, LINE, greet_line, 0)
    pl.semaphore_wait(barrier, PLANE - 1 + LINE - 1)

    gs = Gather(0, sgat, send, recv, row, y, z)
    ge = Gather(1, egat, send, recv, row, y, z)
    ga = Gather(2, agat, send, recv, row, y, z)

    loads[0].wait()
    gs.first_ring(0)
    gs.first_ring(1)
    gs.second_ring(1, 0)
    gs.second_ring(0, 0)

    def plane_copy(k):
        to = (me + k) % PLANE
        return pltpu.make_async_remote_copy(
            src_ref=wrow.at[:, pl.ds(pl.multiple_of(to * width, width), width)],
            dst_ref=wcol.at[me, row],
            send_sem=wsend.at[k],
            recv_sem=wrecv.at[k],
            device_id={"sa": row, "an": to},
            device_id_type=pl.DeviceIdType.MESH,
        )

    def plane_arrival(k):
        return pltpu.make_async_remote_copy(
            src_ref=wcol.at[(me + PLANE - k) % PLANE, row],
            dst_ref=wcol.at[(me + PLANE - k) % PLANE, row],
            send_sem=wsend.at[k],
            recv_sem=wrecv.at[k],
            device_id={"sa": row, "an": (me + k) % PLANE},
            device_id_type=pl.DeviceIdType.MESH,
        )

    def line_copy(k, held):
        return pltpu.make_async_remote_copy(
            src_ref=wcol.at[:, held],
            dst_ref=wcol.at[:, held],
            send_sem=lsend.at[k],
            recv_sem=lrecv.at[k],
            device_id={"sa": (row + k) % LINE, "an": me},
            device_id_type=pl.DeviceIdType.MESH,
        )

    def repeat(first, last, step):
        def one(k, carry):
            step(k)
            return carry

        lax.fori_loop(first, last, one, 0)

    loads[1].wait()
    repeat(1, PLANE, lambda k: plane_copy(k).start())

    loads[2].wait()
    span = pool.shape[1]
    for slot in range(NEIGH):
        rows = pool[table[32 + slot]].astype(F32)
        cut = pl.ds(slot * span, span)
        wide[cut] = rows
        square = jnp.mean(rows * rows, axis=-1, keepdims=True)
        normed[cut] = (rows * lax.rsqrt(square + EPS)).astype(BF16)

    def encode_chunk(f):
        load_up(f).wait()
        load_down(f).wait()
        cut = pl.ds(pl.multiple_of(f * FCHUNK, FCHUNK), FCHUNK)
        pre = jnp.dot(normed[...], up[:, cut], preferred_element_type=F32)
        hidden = (0.5 * pre * (1.0 + lax.erf(pre * 0.5**0.5))).astype(BF16)
        wide[...] += jnp.dot(hidden, down[cut], preferred_element_type=F32)

    repeat(0, 3, encode_chunk)
    gs.event1()
    repeat(3, 6, encode_chunk)
    gs.event2()
    gs.event3()
    loads[6].wait()
    repeat(1, PLANE, lambda k: plane_arrival(k).wait_recv())
    repeat(1, LINE, lambda k: line_copy(k, row).start())
    repeat(6, chunks, encode_chunk)
    egat[me] = wide[...].astype(BF16)
    gs.event4()
    ge.first_ring(0)
    ge.first_ring(1)
    ge.second_ring(1, 0)
    ge.second_ring(0, 0)
    gs.event5()
    loads[4].wait()
    loads[5].wait()

    def project(i, where):
        h, dp, dq = where(i)
        slot = ge.block(h, dp, dq) * NEIGH + h
        cut = pl.ds(pl.multiple_of(h * span, span), span)
        both = jnp.dot(egat[ge.block(h, dp, dq), cut], wkv[...], preferred_element_type=F32)
        keys[slot] = both[:, :width].astype(BF16)
        vals[slot] = both[:, width:].astype(BF16)

    def on_arrival(event, work):
        count, where = ARRIVED[event]
        repeat(0, count, lambda i: work(i, where))

    gs.event6()
    ge.event1()
    loads[3].wait()

    def query_tile(t):
        cut = pl.ds(pl.multiple_of(t * 256, 256), 256)
        acc = jnp.zeros((256, width), F32)
        for j in range(PLANE):
            acc = acc + jnp.dot(
                sgat[j, cut], wq[j * width : (j + 1) * width], preferred_element_type=F32
            )
        qs[cut] = acc.astype(BF16)

    on_arrival(0, project)
    on_arrival(1, project)
    ge.event2()
    on_arrival(2, project)
    ge.event3()
    on_arrival(3, project)
    repeat(0, tokens // 256, query_tile)
    ge.event4()
    on_arrival(4, project)
    ge.event5()
    on_arrival(5, project)
    ge.event6()
    on_arrival(6, project)

    scale = float(HEAD) ** -0.5

    def attend(g):
        cut = pl.ds(pl.multiple_of(g * GROUP, GROUP), GROUP)
        one, two = table[NEIGH * g], table[NEIGH * g + 1]
        k = jnp.concatenate([keys[one], keys[two]], axis=0)
        v = jnp.concatenate([vals[one], vals[two]], axis=0)
        q = qs[cut]
        done = []
        for h in range(width // HEAD):
            part = slice(h * HEAD, (h + 1) * HEAD)
            scores = lax.dot_general(
                q[:, part], k[:, part], (((1,), (1,)), ((), ())), preferred_element_type=F32
            ) * scale
            weights = jnp.exp(scores - jnp.max(scores, axis=-1, keepdims=True))
            probs = weights / jnp.sum(weights, axis=-1, keepdims=True)
            done.append(jnp.dot(probs.astype(BF16), v[:, part], preferred_element_type=F32))
        agat[me, cut] = jnp.concatenate(done, axis=1).astype(BF16)

    groups = tokens // GROUP
    lax.fori_loop(0, groups // 4, lambda g, c: (attend(2 * g), attend(2 * g + 1), c)[2], 0)
    ga.first_ring(0)
    ga.second_ring(0, 0)
    lax.fori_loop(groups // 4, groups // 2, lambda g, c: (attend(2 * g), attend(2 * g + 1), c)[2], 0)
    ga.first_ring(1)
    ga.second_ring(1, 0)

    repeat(1, LINE, lambda k: line_copy(k, (row + LINE - k) % LINE).wait_recv())
    total[...] = jnp.zeros_like(total)

    def add_output(i, where):
        h, dp, dq = where(i)
        j = ga.block(h, dp, dq)
        half = tokens // 2
        cut = pl.ds(pl.multiple_of(h * half, half), half)
        total[cut] += jnp.dot(
            agat[j, cut], wcol[j].reshape(width, width), preferred_element_type=F32
        )

    on_arrival(0, add_output)
    ga.event1()
    on_arrival(1, add_output)
    ga.event2()
    on_arrival(2, add_output)
    ga.event3()
    on_arrival(3, add_output)
    ga.event4()
    on_arrival(4, add_output)
    ga.event5()
    on_arrival(5, add_output)
    ga.event6()
    on_arrival(6, add_output)
    out[...] = total[...].astype(BF16)

    for gather in (gs, ge, ga):
        gather.sent()
    repeat(1, PLANE, lambda k: plane_copy(k).wait_send())
    repeat(1, LINE, lambda k: line_copy(k, row).wait_send())


def request_table(requests, own, position):
    owner = requests // own
    same = owner[:, None] == owner[None, :]
    rank = jnp.any(same & (requests[None, :] < requests[:, None]), axis=1)
    slot = owner * NEIGH + rank.astype(jnp.int32)
    mine = owner == position
    low = jnp.min(jnp.where(mine, requests % own, own - 1))
    high = jnp.max(jnp.where(mine, requests % own, 0))
    return jnp.concatenate([slot, jnp.stack([low, high])]).astype(jnp.int32)


def shards(
    decoder_states, w_query, w_key, w_value, w_out, enc_up, enc_down, neighbour_inputs, requests
):
    tokens, width = decoder_states.shape
    own, span, features = neighbour_inputs.shape
    table = request_table(requests, own, lax.axis_index("an"))
    hbm = pl.BlockSpec(memory_space=pl.ANY)
    slots = PLANE * NEIGH
    chunks = enc_up.shape[1] // FCHUNK
    return pl.pallas_call(
        body,
        out_shape=jax.ShapeDtypeStruct((tokens, width), BF16),
        in_specs=[pl.BlockSpec(memory_space=pltpu.SMEM)] + [hbm] * 8,
        out_specs=pl.BlockSpec(memory_space=pltpu.VMEM),
        scratch_shapes=[
            pltpu.VMEM((PLANE, tokens, width), BF16),
            pltpu.VMEM((PLANE, NEIGH * span, features), BF16),
            pltpu.VMEM((PLANE, tokens, width), BF16),
            pltpu.VMEM((PLANE, LINE, w_out.shape[0] // LINE, width), BF16),
            pltpu.VMEM(w_query.shape, BF16),
            pltpu.VMEM((features, 2 * width), BF16),
            pltpu.VMEM((w_out.shape[0] // LINE, w_out.shape[1]), BF16),
            pltpu.VMEM(enc_up.shape, BF16),
            pltpu.VMEM(enc_down.shape, BF16),
            pltpu.VMEM(neighbour_inputs.shape, BF16),
            pltpu.VMEM((NEIGH * span, features), F32),
            pltpu.VMEM((NEIGH * span, features), BF16),
            pltpu.VMEM((tokens, width), BF16),
            pltpu.VMEM((slots, span, width), BF16),
            pltpu.VMEM((slots, span, width), BF16),
            pltpu.VMEM((tokens, width), F32),
            pltpu.SemaphoreType.DMA((3, 2 * MESSAGES)),
            pltpu.SemaphoreType.DMA((3, 2 * MESSAGES)),
            pltpu.SemaphoreType.DMA((PLANE,)),
            pltpu.SemaphoreType.DMA((PLANE,)),
            pltpu.SemaphoreType.DMA((LINE,)),
            pltpu.SemaphoreType.DMA((LINE,)),
            pltpu.SemaphoreType.DMA((7,)),
            pltpu.SemaphoreType.DMA((2, chunks)),
        ],
        compiler_params=pltpu.CompilerParams(
            collective_id=0, has_side_effects=True, vmem_limit_bytes=67043328
        ),
    )(
        table, decoder_states, w_query, w_key, w_value, w_out, enc_up, enc_down, neighbour_inputs
    )


def solution(mesh):
    placed = (
        P("sa", "an"),
        P(None, "an"),
        P(None, "an"),
        P(None, "an"),
        P("an", None),
        P(),
        P(),
        P(("sa", "an"), None, None),
        P("sa"),
    )
    return jax.shard_map(
        shards, mesh=mesh, in_specs=placed, out_specs=P("sa", "an"), check_vma=False
    )
```

time: 302 us -> 163 us (0.54)
  waiting for transfers between devices: 177 us -> 0 us
  Pallas kernels: 0 us -> 155 us
  matrix products: 46.7 us -> 0 us
  blocking collectives: 37.9 us -> 0 us
  local copies, waits for them, and re-layouts: 22.8 us -> 1.87 us
  between operations: 13.2 us -> 0.02 us
    all_gather x3 -> x0, waiting for transfers between devices: 177 us -> none  [the longest x1 72.4 us: shards(): lax.all_gather(encoded, 'an', axis=0, tiled=True)]
    pallas_call x0 -> x1, Pallas kernels: none -> 155 us  [shards(): pl.pallas_call(body, out_shape=jax.ShapeDtypeStruct((tokens, width), BF16...]
    dot_general x6 -> x0, matrix products: 46.7 us -> none  [the longest x1 17.1 us: encode(): jnp.dot(hidden, enc_down, preferred_element_type=jnp.float32)]
    all_to_all x1 -> x0, blocking collectives: 37.9 us -> none  [shards(): lax.all_to_all(w_out, 'an', split_axis=1, concat_axis=0, tiled=True)]
    slice x3 -> x0, local copies, waits for them, and re-layouts: 9.28 us -> none  [the longest x2 6.87 us: shards(): selected[:, :, :local_width]]
    gather x3 -> x0, local copies, waits for them, and re-layouts: 6.4 us -> none  [the longest x1 5.1 us: shards(): projected[slot_of_request].reshape(groups, NEIGH * span, 2 * local_width)]
  transfers between devices with their start and end apart: 3 -> 0, of which waited for: 3 -> 0; matrix products, arithmetic and copies ran while one was open for 10% -> 0% of each run, Pallas kernels for 0% -> 0%
where the time goes in v1:
time: 163 us; the launch traced here: 161 us
  Pallas kernels  155 us (95%)
  other arithmetic  4.31 us (3%)
  local copies, waits for them, and re-layouts  1.87 us (1%)
    pallas_call x1, Pallas kernels, shards(): pl.pallas_call(body, out_shape=jax.ShapeDtypeStruct((tokens, width), BF16...  155 us

profile of v1, /device:TPU:1, one launch (start us, length us, event | category | flops | bytes accessed | tf_op | source)
XLA Modules:
  0.0 161.2 jit_solution(12425083263167484381)
XLA Ops:
  0.0 1.4 fusion
  1.4 0.9 and_reduce_fusion
  2.3 2.0 %pad_add_fusion.table = s32[34]{0:T(128)} fusion(s32[1]{0:T(128)} %bitcast.1, s32[1]{0:T(128)} %bitcast, s32[32]{0:T(128)S(1)} %convert_add_fusion), kind=kLoop, calls=%fused_computation.10 | loop fusion | flops 68 | bytes 272 | tf_op jit(solution)/shard_map/concatenate | solution.py:378
  4.3 155.0 %shard_map.91 = bf16[1024,256]{1,0:T(8,128)(2,1)} custom-call(s32[34]{0:T(128)} %pad_add_fusion.table, bf16[1024,256]{1,0:T(8,128)(2,1)} %states.1, bf16[4096,256]{1,0:T(8,128)(2,1)} %w_query.1, bf16[1024,256]{1,0:T(8,128)(2,1)} %w_key.1, bf16[1024,256]{1,0:T(8,128)(2,1)} %w_value.1, bf16[256,4096]{1,0:T(8,128)(2,1)} %w_out.1, bf16[1024,4096]{1,0:T(8,128)(2,1)} %enc_up.1, ...), custom_call_target="tpu_custom_call" | custom-call | tf_op jit(solution)/shard_map/pallas_call | solution.py:390
  159.4 1.9 %copy.11 = bf16[1024,256]{1,0:T(8,128)(2,1)} copy(bf16[1024,256]{1,0:T(8,128)(2,1)} %shard_map.91) | data formatting | bytes 1048576
  (1 shorter events, 0.0 us)

commit v2 on v0

v2 whole, which is shorter than its diff:
```python
import functools

import jax
import jax.numpy as jnp
from jax import lax
from jax.experimental import pallas as pl
from jax.experimental.pallas import tpu as pltpu
from jax.sharding import PartitionSpec as P

HEAD = 128
GROUP = 64
NEIGH = 2
EPS = 1e-06
SIDE = 4
PLANE = SIDE * SIDE
LINE = 8
FCHUNK = 512
CORES = 2
PAIR = 2
F32 = jnp.float32
BF16 = jnp.bfloat16


class Gather:
    def __init__(self, number, buf, send, recv, place):
        self.number, self.buf, self.send, self.recv = number, buf, send, recv
        self.place = place
        self.half = buf.shape[1] // 2

    def copy(self, lane, h, k, dy, db, part, to):
        rows = self.half
        first = h * rows
        if part is not None:
            rows = rows // 2
            first += part * rows
        ref = self.buf.at[self.place.block(lane, dy, db), pl.ds(first, rows)]
        return pltpu.make_async_remote_copy(
            src_ref=ref,
            dst_ref=ref,
            send_sem=self.send.at[self.number, k],
            recv_sem=self.recv.at[self.number, k],
            device_id=to,
            device_id_type=pl.DeviceIdType.MESH,
        )

    def message(self, name, i=0):
        p = self.place
        up, dn, pair = p.ring(1), p.ring(3), p.pair
        if name == "a_up":
            return 0, 0, (0, 0), (3, 0), None, up
        if name == "a_dn":
            return 0, 1, (0, 0), (1, 0), None, dn
        if name == "a_up2":
            return 0, 2, (3, 0), (2, 0), 0, up
        if name == "a_dn2":
            return 0, 3, (1, 0), (2, 0), 1, dn
        if name == "a_pair":
            return 0, 4 + i, (i, 0), (i, 1), None, pair
        if name == "b_pair":
            return 1, 8, (0, 0), (0, 1), None, pair
        if name == "b_up":
            return 1, 9 + i, (0, i), (3, i), None, up
        if name == "b_dn":
            return 1, 11 + i, (0, i), (1, i), None, dn
        if name == "b_up2":
            return 1, 13 + i, (3, i), (2, i), 0, up
        assert name == "b_dn2"
        return 1, 15 + i, (1, i), (2, i), 1, dn

    def go(self, name, i=0):
        h, k, sent, _, part, to = self.message(name, i)
        self.copy(0, h, k, *sent, part, to).start()

    def get(self, name, i=0):
        h, k, _, got, part, to = self.message(name, i)
        self.copy(0, h, k, *got, part, to).wait_recv()

    def across(self, lane, unit):
        h, dy, db = unit
        k = ROUTED + h * 8 + dy * PAIR + db
        return self.copy(lane, h, k, dy, db, None, self.place.twin)

    def share(self, units):
        for unit in units:
            self.across(0, unit).start()

    def shared(self, event):
        for unit in UNITS[event]:
            self.across(1, unit).wait_recv()

    def own(self, h):
        if h == 0:
            self.go("a_up")
            self.go("a_dn")
            self.go("a_pair", 0)
        else:
            self.go("b_pair")
            self.go("b_up", 0)
            self.go("b_dn", 0)
        self.share([UNITS[0][h]])

    def event(self, e):
        if e == 1:
            self.get("a_up")
            self.go("a_up2")
            self.go("a_pair", 3)
            self.get("a_dn")
            self.go("a_dn2")
            self.go("a_pair", 1)
            self.get("b_pair")
            self.go("b_up", 1)
            self.go("b_dn", 1)
        elif e == 2:
            self.get("b_up", 0)
            self.go("b_up2", 0)
            self.get("b_dn", 0)
            self.go("b_dn2", 0)
            self.get("a_pair", 0)
        elif e == 3:
            self.get("a_up2")
            self.get("a_dn2")
            self.go("a_pair", 2)
        elif e == 4:
            self.get("b_up", 1)
            self.go("b_up2", 1)
            self.get("b_dn", 1)
            self.go("b_dn2", 1)
        elif e == 5:
            self.get("a_pair", 3)
            self.get("a_pair", 1)
        else:
            for i in (0, 1):
                self.get("b_up2", i)
                self.get("b_dn2", i)
            self.get("a_pair", 2)
        self.share(UNITS[e])

    def sent(self):
        for name, count in MESSAGES:
            for i in range(count):
                h, k, sent, _, part, to = self.message(name, i)
                self.copy(0, h, k, *sent, part, to).wait_send()
        for event in UNITS:
            for unit in UNITS[event]:
                self.across(0, unit).wait_send()


MESSAGES = (
    ("a_up", 1), ("a_dn", 1), ("a_up2", 1), ("a_dn2", 1), ("a_pair", 4),
    ("b_pair", 1), ("b_up", 2), ("b_dn", 2), ("b_up2", 2), ("b_dn2", 2),
)
ROUTED = 17
SWAP = 33
UNITS = {
    0: [(0, 0, 0), (1, 0, 0)],
    1: [(0, 3, 0), (0, 1, 0), (1, 0, 1)],
    2: [(1, 3, 0), (1, 1, 0), (0, 0, 1)],
    3: [(0, 2, 0)],
    4: [(1, 3, 1), (1, 1, 1)],
    5: [(0, 3, 1), (0, 1, 1)],
    6: [(1, 2, 0), (1, 2, 1), (0, 2, 1)],
}


class Place:
    def __init__(self):
        self.row = lax.axis_index("sa")
        self.me = lax.axis_index("an")
        self.x, self.c = self.row // CORES, self.row % CORES
        self.y, self.z = self.me // SIDE, self.me % SIDE
        self.s, self.b = self.z // PAIR, self.z % PAIR
        self.foreign = (self.c + self.s) % 2
        self.outer = self.y * SIDE + self.outer_z(self.z)
        self.mine = self.block(0, 0, 0)
        self.pair = {"sa": self.row, "an": self.y * SIDE + self.s * PAIR + 1 - self.b}
        self.twin = {"sa": self.row + 1 - 2 * self.c, "an": self.me}
        self.partner = {"sa": self.row + 1 - 2 * self.c, "an": self.outer}
        self.holder = {"sa": self.row, "an": self.outer}

    def outer_z(self, z):
        return (z + 2 * (z % PAIR) + 3) % SIDE

    def ring(self, dy):
        return {"sa": self.row, "an": ((self.y + dy) % SIDE) * SIDE + self.z}

    def block(self, lane, dy, db):
        foreign = (self.foreign + lane) % 2
        b = (self.b + db) % PAIR
        z = self.s * PAIR + b
        return ((self.y + dy) % SIDE) * SIDE + (z + foreign * (2 * b + 3)) % SIDE

    def task_of(self, an):
        y, z = an // SIDE, an % SIDE
        foreign = (self.c + z // PAIR) % 2
        return y * SIDE + (z + foreign * (2 * (z % PAIR) + 3)) % SIDE


def repeat(first, last, step):
    def one(k, carry):
        step(k)
        return carry

    lax.fori_loop(first, last, one, 0)


def either(flag, yes, no):
    pl.when(flag == 1)(yes)
    pl.when(flag == 0)(no)


def visit(own, shared, work):
    units = [(0,) + unit for unit in own] + [(1,) + unit for unit in shared]

    def one(i):
        picked = []
        for column in zip(*units):
            value = jnp.int32(column[0])
            for k in range(1, len(column)):
                value = jnp.where(i == k, jnp.int32(column[k]), value)
            picked.append(value)
        work(*picked)

    repeat(0, len(units), one)


def body(
    table, states, w_query, w_key, w_value, w_out, enc_up, enc_down, nearby, out,
    sgat, egat, agat, wcol, wq, wkv, wrow, up, down, pool,
    wide, normed, qs, keys, vals, total, arrived, other_table, local_table, task_table,
    send, recv, wsend, wrecv, lsend, lrecv, qsend, qrecv, local, wsem,
):
    p = Place()
    row, me, x, b = p.row, p.me, p.x, p.b
    tokens, width = states.shape
    wrows = w_out.shape[0] // LINE
    chunks = enc_up.shape[1] // FCHUNK
    share = x * PAIR + b

    def remote(src, dst, ssem, rsem, to):
        return pltpu.make_async_remote_copy(
            src_ref=src, dst_ref=dst, send_sem=ssem, recv_sem=rsem,
            device_id=to, device_id_type=pl.DeviceIdType.MESH,
        )

    load_states = pltpu.make_async_copy(states, sgat.at[me], local.at[0])
    load_rows = pltpu.make_async_copy(
        w_out.at[pl.ds(x * PAIR * wrows, PAIR * wrows)], wrow, local.at[1]
    )
    load_pool = pltpu.make_async_copy(nearby, pool, local.at[2])
    load_query = pltpu.make_async_copy(w_query, wq, local.at[3])
    load_key = pltpu.make_async_copy(w_key, wkv.at[:, pl.ds(0, width)], local.at[4])
    load_value = pltpu.make_async_copy(w_value, wkv.at[:, pl.ds(width, width)], local.at[5])
    load_column = pltpu.make_async_copy(
        w_out.at[
            pl.ds(pl.multiple_of(share * wrows, wrows), wrows),
            pl.ds(pl.multiple_of(p.mine * width, width), width),
        ],
        wcol.at[me, share],
        local.at[6],
    )
    load_table = pltpu.make_async_copy(table, local_table, local.at[7])

    def load_up(f):
        cut = pl.ds(pl.multiple_of(f * FCHUNK, FCHUNK), FCHUNK)
        return pltpu.make_async_copy(enc_up.at[:, cut], up.at[:, cut], wsem.at[0, f])

    def load_down(f):
        cut = pl.ds(pl.multiple_of(f * FCHUNK, FCHUNK), FCHUNK)
        return pltpu.make_async_copy(enc_down.at[cut], down.at[cut], wsem.at[1, f])

    def load_weights():
        load_key.start()
        load_value.start()
        load_query.start()

    pl.when(p.foreign == 0)(load_states.start)
    load_table.start()
    load_pool.start()
    load_rows.start()
    load_column.start()
    repeat(0, chunks, lambda f: (load_up(f).start(), load_down(f).start()))
    pl.when(p.foreign == 0)(load_weights)

    barrier = pltpu.get_barrier_semaphore()

    def greet(to):
        pl.semaphore_signal(barrier, inc=1, device_id=to, device_id_type=pl.DeviceIdType.MESH)

    def line(k):
        far = k % PAIR
        at = far * p.outer + (1 - far) * me
        return {"sa": ((x + k // PAIR) % SIDE) * CORES + p.c, "an": at}

    greet(p.partner)
    greet(p.twin)
    repeat(1, PLANE, lambda k: greet({"sa": row, "an": (me + k) % PLANE}))
    repeat(1, LINE, lambda k: greet(line(k)))
    pl.semaphore_wait(barrier, PLANE - 1 + LINE - 1 + 2)

    gs = Gather(0, sgat, send, recv, p)
    ge = Gather(1, egat, send, recv, p)
    ga = Gather(2, agat, send, recv, p)

    def swap(number, src, buf, to_slot):
        return remote(
            src, buf.at[to_slot], send.at[number, SWAP], recv.at[number, SWAP], p.partner
        )

    def swap_states():
        swap(0, states, sgat, me).start()
        swap(0, states, sgat, p.outer).wait_recv()

    either(p.foreign, swap_states, load_states.wait)
    gs.own(1)
    gs.own(0)

    table_copy = remote(table, other_table, qsend.at[0], qrecv.at[0], p.twin)
    table_copy.start()

    def plane_copy(k):
        an = (me + k) % PLANE
        part = an % PAIR
        task = p.task_of(an)
        return remote(
            wrow.at[
                pl.ds(pl.multiple_of(part * wrows, wrows), wrows),
                pl.ds(pl.multiple_of(task * width, width), width),
            ],
            wcol.at[me, x * PAIR + part],
            wsend.at[k],
            wrecv.at[k],
            {"sa": row, "an": an},
        )

    def plane_arrival(k):
        ref = wcol.at[(me + PLANE - k) % PLANE, share]
        return remote(ref, ref, wsend.at[k], wrecv.at[k], {"sa": row, "an": (me + k) % PLANE})

    def line_copy(k, held):
        ref = wcol.at[:, held]
        return remote(ref, ref, lsend.at[k], lrecv.at[k], line(k))

    def line_arrival(k):
        far = k % PAIR
        part = b + far * (1 - 2 * b)
        return line_copy(k, ((x + SIDE - k // PAIR) % SIDE) * PAIR + part)

    load_rows.wait()
    repeat(1, PLANE, lambda k: plane_copy(k).start())

    load_table.wait()
    load_pool.wait()
    span = pool.shape[1]
    for slot in range(NEIGH):
        rows = pool[local_table[0, 32 + slot]].astype(F32)
        cut = pl.ds(slot * span, span)
        wide[cut] = rows
        square = jnp.mean(rows * rows, axis=-1, keepdims=True)
        normed[cut] = (rows * lax.rsqrt(square + EPS)).astype(BF16)

    def encode_chunk(f):
        load_up(f).wait()
        load_down(f).wait()
        cut = pl.ds(pl.multiple_of(f * FCHUNK, FCHUNK), FCHUNK)
        pre = jnp.dot(normed[...], up[:, cut], preferred_element_type=F32)
        hidden = (0.5 * pre * (1.0 + lax.erf(pre * 0.5**0.5))).astype(BF16)
        wide[...] += jnp.dot(hidden, down[cut], preferred_element_type=F32)

    weight_copies = (
        remote(wkv, wkv, qsend.at[1], qrecv.at[1], p.holder),
        remote(wq, wq, qsend.at[2], qrecv.at[2], p.holder),
    )

    def give_weights():
        load_key.wait()
        load_value.wait()
        load_query.wait()
        for copy in weight_copies:
            copy.start()

    repeat(0, 2, encode_chunk)
    gs.event(1)
    pl.when(p.foreign == 0)(give_weights)
    repeat(2, 4, encode_chunk)
    gs.event(2)
    gs.event(3)
    repeat(4, 6, encode_chunk)
    gs.event(4)
    repeat(6, chunks, encode_chunk)

    def swap_encoded():
        normed[...] = wide[...].astype(BF16)
        swap(1, normed, egat, me).start()

    def keep_encoded():
        egat[me] = wide[...].astype(BF16)

    either(p.foreign, swap_encoded, keep_encoded)
    gs.event(5)
    pl.when(p.foreign == 1)(swap(1, normed, egat, p.outer).wait_recv)
    ge.own(1)
    ge.own(0)
    load_column.wait()
    repeat(1, PLANE, lambda k: plane_arrival(k).wait_recv())
    repeat(1, LINE, lambda k: line_copy(k, share).start())
    gs.event(6)

    def task_table_from(src):
        def copy():
            moved = pltpu.make_async_copy(src, task_table, local.at[8])
            moved.start()
            moved.wait()

        return copy

    table_copy.wait_recv()
    either(p.foreign, task_table_from(other_table), task_table_from(table))
    pl.when(p.foreign == 1)(weight_copies[0].wait_recv)

    def project(lane, h, dy, db):
        block = p.block(lane, dy, db)
        slot = block * NEIGH + h
        cut = pl.ds(pl.multiple_of(h * span, span), span)
        both = jnp.dot(egat[block, cut], wkv[...], preferred_element_type=F32)
        keys[slot] = both[:, :width].astype(BF16)
        vals[slot] = both[:, width:].astype(BF16)

    def query_tile(t):
        cut = pl.ds(pl.multiple_of(t * 256, 256), 256)
        acc = jnp.zeros((256, width), F32)
        for j in range(PLANE):
            acc = acc + jnp.dot(
                sgat[j, cut], wq[j * width : (j + 1) * width], preferred_element_type=F32
            )
        qs[cut] = acc.astype(BF16)

    ge.event(1)
    ge.shared(0)
    visit(UNITS[0] + UNITS[1], UNITS[0], project)
    ge.event(2)
    ge.shared(1)
    visit(UNITS[2], UNITS[1], project)
    ge.event(3)
    ge.shared(2)
    visit(UNITS[3], UNITS[2], project)
    for event in UNITS:
        gs.shared(event)
    pl.when(p.foreign == 1)(weight_copies[1].wait_recv)
    ge.event(4)
    repeat(0, tokens // 256, query_tile)
    ge.shared(3)
    visit(UNITS[4], UNITS[3], project)
    ge.event(5)
    ge.shared(4)
    visit(UNITS[5], UNITS[4], project)
    ge.event(6)
    ge.shared(5)
    visit(UNITS[6], UNITS[5], project)
    ge.shared(6)
    visit([], UNITS[6], project)

    scale = float(HEAD) ** -0.5

    def attend(g):
        cut = pl.ds(pl.multiple_of(g * GROUP, GROUP), GROUP)
        one, two = task_table[0, NEIGH * g], task_table[0, NEIGH * g + 1]
        k = jnp.concatenate([keys[one], keys[two]], axis=0)
        v = jnp.concatenate([vals[one], vals[two]], axis=0)
        q = qs[cut]
        done = []
        for h in range(width // HEAD):
            part = slice(h * HEAD, (h + 1) * HEAD)
            scores = lax.dot_general(
                q[:, part], k[:, part], (((1,), (1,)), ((), ())), preferred_element_type=F32
            ) * scale
            weights = jnp.exp(scores - jnp.max(scores, axis=-1, keepdims=True))
            probs = weights / jnp.sum(weights, axis=-1, keepdims=True)
            done.append(jnp.dot(probs.astype(BF16), v[:, part], preferred_element_type=F32))
        agat[p.mine, cut] = jnp.concatenate(done, axis=1).astype(BF16)

    pairs = tokens // GROUP // 2
    repeat(0, pairs // 2, lambda g: (attend(2 * g), attend(2 * g + 1)))
    ga.own(0)
    repeat(pairs // 2, pairs, lambda g: (attend(2 * g), attend(2 * g + 1)))
    ga.own(1)

    repeat(1, LINE, lambda k: line_arrival(k).wait_recv())
    total[...] = jnp.zeros_like(total)

    def add_output(lane, h, dy, db):
        j = p.block(lane, dy, db)
        half = tokens // 2
        cut = pl.ds(pl.multiple_of(h * half, half), half)
        total[cut] += jnp.dot(
            agat[j, cut], wcol[j].reshape(width, width), preferred_element_type=F32
        )

    visit(UNITS[0], [], add_output)
    for event in range(1, 7):
        ga.event(event)
        ga.shared(event - 1)
        visit(UNITS[event], UNITS[event - 1], add_output)
    ga.shared(6)
    visit([], UNITS[6], add_output)

    swap_out = remote(qs, arrived, send.at[2, SWAP], recv.at[2, SWAP], p.partner)

    def swap_output():
        qs[...] = total[...].astype(BF16)
        swap_out.start()
        swap_out.wait_recv()
        out[...] = arrived[...]

    def keep_output():
        out[...] = total[...].astype(BF16)

    either(p.foreign, swap_output, keep_output)

    for gather in (gs, ge, ga):
        gather.sent()
    table_copy.wait_send()

    def sent_foreign():
        swap(0, states, sgat, me).wait_send()
        swap(1, normed, egat, me).wait_send()
        swap_out.wait_send()

    def sent_home():
        for copy in weight_copies:
            copy.wait_send()

    either(p.foreign, sent_foreign, sent_home)
    repeat(1, PLANE, lambda k: plane_copy(k).wait_send())
    repeat(1, LINE, lambda k: line_copy(k, share).wait_send())


def request_table(requests, own, position):
    owner = requests // own
    same = owner[:, None] == owner[None, :]
    rank = jnp.any(same & (requests[None, :] < requests[:, None]), axis=1)
    slot = owner * NEIGH + rank.astype(jnp.int32)
    mine = owner == position
    low = jnp.min(jnp.where(mine, requests % own, own - 1))
    high = jnp.max(jnp.where(mine, requests % own, 0))
    packed = jnp.concatenate([slot, jnp.stack([low, high])]).astype(jnp.int32)
    return jnp.pad(packed, (0, HEAD - packed.shape[0]))[None, :]


def shards(
    decoder_states, w_query, w_key, w_value, w_out, enc_up, enc_down, neighbour_inputs, requests
):
    tokens, width = decoder_states.shape
    own, span, features = neighbour_inputs.shape
    table = request_table(requests, own, lax.axis_index("an"))
    hbm = pl.BlockSpec(memory_space=pl.ANY)
    slots = PLANE * NEIGH
    chunks = enc_up.shape[1] // FCHUNK
    return pl.pallas_call(
        body,
        out_shape=jax.ShapeDtypeStruct((tokens, width), BF16),
        in_specs=[pl.BlockSpec(memory_space=pltpu.VMEM)] + [hbm] * 8,
        out_specs=pl.BlockSpec(memory_space=pltpu.VMEM),
        scratch_shapes=[
            pltpu.VMEM((PLANE, tokens, width), BF16),
            pltpu.VMEM((PLANE, NEIGH * span, features), BF16),
            pltpu.VMEM((PLANE, tokens, width), BF16),
            pltpu.VMEM((PLANE, LINE, w_out.shape[0] // LINE, width), BF16),
            pltpu.VMEM(w_query.shape, BF16),
            pltpu.VMEM((features, 2 * width), BF16),
            pltpu.VMEM((PAIR * w_out.shape[0] // LINE, w_out.shape[1]), BF16),
            pltpu.VMEM(enc_up.shape, BF16),
            pltpu.VMEM(enc_down.shape, BF16),
            pltpu.VMEM(neighbour_inputs.shape, BF16),
            pltpu.VMEM((NEIGH * span, features), F32),
            pltpu.VMEM((NEIGH * span, features), BF16),
            pltpu.VMEM((tokens, width), BF16),
            pltpu.VMEM((slots, span, width), BF16),
            pltpu.VMEM((slots, span, width), BF16),
            pltpu.VMEM((tokens, width), F32),
            pltpu.VMEM((tokens, width), BF16),
            pltpu.VMEM((1, HEAD), jnp.int32),
            pltpu.SMEM((1, HEAD), jnp.int32),
            pltpu.SMEM((1, HEAD), jnp.int32),
            pltpu.SemaphoreType.DMA((3, SWAP + 1)),
            pltpu.SemaphoreType.DMA((3, SWAP + 1)),
            pltpu.SemaphoreType.DMA((PLANE,)),
            pltpu.SemaphoreType.DMA((PLANE,)),
            pltpu.SemaphoreType.DMA((LINE,)),
            pltpu.SemaphoreType.DMA((LINE,)),
            pltpu.SemaphoreType.DMA((3,)),
            pltpu.SemaphoreType.DMA((3,)),
            pltpu.SemaphoreType.DMA((9,)),
            pltpu.SemaphoreType.DMA((2, chunks)),
        ],
        compiler_params=pltpu.CompilerParams(
            collective_id=0, has_side_effects=True, vmem_limit_bytes=67043328
        ),
    )(
        table, decoder_states, w_query, w_key, w_value, w_out, enc_up, enc_down, neighbour_inputs
    )


def solution(mesh):
    placed = (
        P("sa", "an"),
        P(None, "an"),
        P(None, "an"),
        P(None, "an"),
        P("an", None),
        P(),
        P(),
        P(("sa", "an"), None, None),
        P("sa"),
    )
    return jax.shard_map(
        shards, mesh=mesh, in_specs=placed, out_specs=P("sa", "an"), check_vma=False
    )
```

time: 302 us -> 147 us (0.49)
  waiting for transfers between devices: 177 us -> 0 us
  Pallas kernels: 0 us -> 140 us
  matrix products: 46.7 us -> 0 us
  blocking collectives: 37.9 us -> 0 us
  local copies, waits for them, and re-layouts: 22.8 us -> 2.39 us
  between operations: 13.2 us -> 0.02 us
    all_gather x3 -> x0, waiting for transfers between devices: 177 us -> none  [the longest x1 72.4 us: shards(): lax.all_gather(encoded, 'an', axis=0, tiled=True)]
    pallas_call x0 -> x1, Pallas kernels: none -> 140 us  [shards(): pl.pallas_call(body, out_shape=jax.ShapeDtypeStruct((tokens, width), BF16...]
    dot_general x6 -> x0, matrix products: 46.7 us -> none  [the longest x1 17.1 us: encode(): jnp.dot(hidden, enc_down, preferred_element_type=jnp.float32)]
    all_to_all x1 -> x0, blocking collectives: 37.9 us -> none  [shards(): lax.all_to_all(w_out, 'an', split_axis=1, concat_axis=0, tiled=True)]
    slice x3 -> x0, local copies, waits for them, and re-layouts: 9.28 us -> none  [the longest x2 6.87 us: shards(): selected[:, :, :local_width]]
    gather x3 -> x0, local copies, waits for them, and re-layouts: 6.4 us -> none  [the longest x1 5.1 us: shards(): projected[slot_of_request].reshape(groups, NEIGH * span, 2 * local_width)]
  transfers between devices with their start and end apart: 3 -> 0, of which waited for: 3 -> 0; matrix products, arithmetic and copies ran while one was open for 10% -> 0% of each run, Pallas kernels for 0% -> 0%
where the time goes in v2:
time: 147 us; the launch traced here: 146 us
  Pallas kernels  140 us (95%)
  other arithmetic  3.72 us (3%)
  local copies, waits for them, and re-layouts  2.39 us (2%)
    pallas_call x1, Pallas kernels, shards(): pl.pallas_call(body, out_shape=jax.ShapeDtypeStruct((tokens, width), BF16...  140 us

profile of v2, /device:TPU:1, one launch (start us, length us, event | category | flops | bytes accessed | tf_op | source)
XLA Modules:
  0.0 146.3 jit_solution(2927577465146985999)
XLA Ops:
  0.0 1.4 fusion
  1.4 0.9 and_reduce_fusion
  2.3 1.4 pad_add_fusion
  3.7 0.5 pad_bitcast_fusion.table
  4.2 140.2 %shard_map.91 = bf16[1024,256]{1,0:T(8,128)(2,1)} custom-call(s32[1,128]{1,0:T(1,128)} %pad_bitcast_fusion.table, bf16[1024,256]{1,0:T(8,128)(2,1)} %states.1, bf16[4096,256]{1,0:T(8,128)(2,1)} %w_query.1, bf16[1024,256]{1,0:T(8,128)(2,1)} %w_key.1, bf16[1024,256]{1,0:T(8,128)(2,1)} %w_value.1, bf16[256,4096]{1,0:T(8,128)(2,1)} %w_out.1, ...), custom_call_target="tpu_custom_call" | custom-call | tf_op jit(solution)/shard_map/pallas_call | solution.py:558
  144.5 1.9 %copy.11 = bf16[1024,256]{1,0:T(8,128)(2,1)} copy(bf16[1024,256]{1,0:T(8,128)(2,1)} %shard_map.91) | data formatting | bytes 1048576
  (1 shorter events, 0.0 us)

commit v3 on v2

--- a/solution.py
+++ b/solution.py
@@ -17,6 +17,7 @@
 FCHUNK = 512
 CORES = 2
 PAIR = 2
+LOG2E = 1.4426950408889634
 F32 = jnp.float32
 BF16 = jnp.bfloat16
 
@@ -98,6 +99,15 @@
             self.go("b_up", 0)
             self.go("b_dn", 0)
         self.share([UNITS[0][h]])
+
+    def own_both(self):
+        self.go("b_pair")
+        self.go("a_up")
+        self.go("a_dn")
+        self.go("a_pair", 0)
+        self.go("b_up", 0)
+        self.go("b_dn", 0)
+        self.share(UNITS[0])
 
     def event(self, e):
         if e == 1:
@@ -128,10 +138,11 @@
         elif e == 5:
             self.get("a_pair", 3)
             self.get("a_pair", 1)
-        else:
+        elif e == 6:
             for i in (0, 1):
                 self.get("b_up2", i)
                 self.get("b_dn2", i)
+        else:
             self.get("a_pair", 2)
         self.share(UNITS[e])
 
@@ -158,7 +169,8 @@
     3: [(0, 2, 0)],
     4: [(1, 3, 1), (1, 1, 1)],
     5: [(0, 3, 1), (0, 1, 1)],
-    6: [(1, 2, 0), (1, 2, 1), (0, 2, 1)],
+    6: [(1, 2, 0), (1, 2, 1)],
+    7: [(0, 2, 1)],
 }
 
 
@@ -224,9 +236,9 @@
 
 
 def body(
-    table, states, w_query, w_key, w_value, w_out, enc_up, enc_down, nearby, out,
+    mine_req, table, states, w_query, w_key, w_value, w_out, enc_up, enc_down, nearby, out,
     sgat, egat, agat, wcol, wq, wkv, wrow, up, down, pool,
-    wide, normed, qs, keys, vals, total, arrived, other_table, local_table, task_table,
+    wide, normed, qs, keys, vals, total, arrived, other_table, task_req, slots,
     send, recv, wsend, wrecv, lsend, lrecv, qsend, qrecv, local, wsem,
 ):
     p = Place()
@@ -243,6 +255,7 @@
         )
 
     load_states = pltpu.make_async_copy(states, sgat.at[me], local.at[0])
+    stage_states = pltpu.make_async_copy(states, qs, local.at[0])
     load_rows = pltpu.make_async_copy(
         w_out.at[pl.ds(x * PAIR * wrows, PAIR * wrows)], wrow, local.at[1]
     )
@@ -258,7 +271,6 @@
         wcol.at[me, share],
         local.at[6],
     )
-    load_table = pltpu.make_async_copy(table, local_table, local.at[7])
 
     def load_up(f):
         cut = pl.ds(pl.multiple_of(f * FCHUNK, FCHUNK), FCHUNK)
@@ -273,14 +285,6 @@
         load_value.start()
         load_query.start()
 
-    pl.when(p.foreign == 0)(load_states.start)
-    load_table.start()
-    load_pool.start()
-    load_rows.start()
-    load_column.start()
-    repeat(0, chunks, lambda f: (load_up(f).start(), load_down(f).start()))
-    pl.when(p.foreign == 0)(load_weights)
-
     barrier = pltpu.get_barrier_semaphore()
 
     def greet(to):
@@ -295,27 +299,81 @@
     greet(p.twin)
     repeat(1, PLANE, lambda k: greet({"sa": row, "an": (me + k) % PLANE}))
     repeat(1, LINE, lambda k: greet(line(k)))
+
+    load_pool.start()
+    repeat(0, chunks // 2, lambda f: (load_up(f).start(), load_down(f).start()))
+    either(p.foreign, stage_states.start, load_states.start)
+    repeat(chunks // 2, chunks, lambda f: (load_up(f).start(), load_down(f).start()))
+    load_rows.start()
+    load_column.start()
+    pl.when(p.foreign == 0)(load_weights)
+
+    span, own = pool.shape[1], pool.shape[0]
+    requests = mine_req.shape[0]
+    low, high = jnp.int32(own - 1), jnp.int32(0)
+    for k in range(requests):
+        offset = mine_req[k] - me * own
+        here = (offset >= 0) & (offset < own)
+        low = jnp.where(here, jnp.minimum(low, offset), low)
+        high = jnp.where(here, jnp.maximum(high, offset), high)
+    load_pool.wait()
+    for slot, chosen in enumerate((low, high)):
+        rows = pool[chosen].astype(F32)
+        cut = pl.ds(slot * span, span)
+        wide[cut] = rows
+        square = jnp.mean(rows * rows, axis=-1, keepdims=True)
+        normed[cut] = (rows * lax.rsqrt(square + EPS)).astype(BF16)
+
+    def encode_chunk(f):
+        load_up(f).wait()
+        load_down(f).wait()
+        cut = pl.ds(pl.multiple_of(f * FCHUNK, FCHUNK), FCHUNK)
+        pre = jnp.dot(normed[...], up[:, cut], preferred_element_type=F32)
+        hidden = (0.5 * pre * (1.0 + lax.erf(pre * 0.5**0.5))).astype(BF16)
+        wide[...] += jnp.dot(hidden, down[cut], preferred_element_type=F32)
+
+    early = 3
+    repeat(0, early, encode_chunk)
     pl.semaphore_wait(barrier, PLANE - 1 + LINE - 1 + 2)
 
     gs = Gather(0, sgat, send, recv, p)
     ge = Gather(1, egat, send, recv, p)
     ga = Gather(2, agat, send, recv, p)
 
-    def swap(number, src, buf, to_slot):
+    def swap(number, h, src, buf, to_slot):
+        cut = pl.ds(h * (buf.shape[1] // 2), buf.shape[1] // 2)
         return remote(
-            src, buf.at[to_slot], send.at[number, SWAP], recv.at[number, SWAP], p.partner
+            src.at[cut], buf.at[to_slot, cut],
+            send.at[number, SWAP + h], recv.at[number, SWAP + h], p.partner,
         )
 
+    def home_states():
+        load_states.wait()
+        gs.own_both()
+
     def swap_states():
-        swap(0, states, sgat, me).start()
-        swap(0, states, sgat, p.outer).wait_recv()
-
-    either(p.foreign, swap_states, load_states.wait)
-    gs.own(1)
-    gs.own(0)
-
+        stage_states.wait()
+        for h in (0, 1):
+            swap(0, h, qs, sgat, me).start()
+
+    either(p.foreign, swap_states, home_states)
     table_copy = remote(table, other_table, qsend.at[0], qrecv.at[0], p.twin)
     table_copy.start()
+    repeat(early, chunks, encode_chunk)
+
+    def swap_encoded():
+        normed[...] = wide[...].astype(BF16)
+        for h in (0, 1):
+            swap(1, h, normed, egat, me).start()
+        for h in (0, 1):
+            swap(0, h, qs, sgat, p.outer).wait_recv()
+            gs.own(h)
+
+    def keep_encoded():
+        egat[me] = wide[...].astype(BF16)
+        ge.own_both()
+
+    either(p.foreign, swap_encoded, keep_encoded)
 
     def plane_copy(k):
         an = (me + k) % PLANE
@@ -345,27 +403,6 @@
         part = b + far * (1 - 2 * b)
         return line_copy(k, ((x + SIDE - k // PAIR) % SIDE) * PAIR + part)
 
-    load_rows.wait()
-    repeat(1, PLANE, lambda k: plane_copy(k).start())
-
-    load_table.wait()
-    load_pool.wait()
-    span = pool.shape[1]
-    for slot in range(NEIGH):
-        rows = pool[local_table[0, 32 + slot]].astype(F32)
-        cut = pl.ds(slot * span, span)
-        wide[cut] = rows
-        square = jnp.mean(rows * rows, axis=-1, keepdims=True)
-        normed[cut] = (rows * lax.rsqrt(square + EPS)).astype(BF16)
-
-    def encode_chunk(f):
-        load_up(f).wait()
-        load_down(f).wait()
-        cut = pl.ds(pl.multiple_of(f * FCHUNK, FCHUNK), FCHUNK)
-        pre = jnp.dot(normed[...], up[:, cut], preferred_element_type=F32)
-        hidden = (0.5 * pre * (1.0 + lax.erf(pre * 0.5**0.5))).astype(BF16)
-        wide[...] += jnp.dot(hidden, down[cut], preferred_element_type=F32)
-
     weight_copies = (
         remote(wkv, wkv, qsend.at[1], qrecv.at[1], p.holder),
         remote(wq, wq, qsend.at[2], qrecv.at[2], p.holder),
@@ -378,43 +415,41 @@
         for copy in weight_copies:
             copy.start()
 
-    repeat(0, 2, encode_chunk)
+    def late_encoded():
+        for h in (0, 1):
+            swap(1, h, normed, egat, p.outer).wait_recv()
+            ge.own(h)
+
+    pl.when(p.foreign == 1)(late_encoded)
     gs.event(1)
+    load_rows.wait()
+    repeat(1, PLANE, lambda k: plane_copy(k).start())
+    table_copy.wait_recv()
+    task_copies = [
+        pltpu.make_async_copy(src, task_req, local.at[7]) for src in (other_table, table)
+    ]
+    either(p.foreign, task_copies[0].start, task_copies[1].start)
+
+    def find_slot(k):
+        wanted = task_req[0, k]
+        owner = wanted // own
+        later = jnp.int32(0)
+        for j in range(requests):
+            other = task_req[0, j]
+            later = jnp.where((other < wanted) & (other >= owner * own), jnp.int32(1), later)
+        slots[k] = owner * NEIGH + later
+
+    gs.event(2)
     pl.when(p.foreign == 0)(give_weights)
-    repeat(2, 4, encode_chunk)
-    gs.event(2)
+    ge.event(1)
     gs.event(3)
-    repeat(4, 6, encode_chunk)
-    gs.event(4)
-    repeat(6, chunks, encode_chunk)
-
-    def swap_encoded():
-        normed[...] = wide[...].astype(BF16)
-        swap(1, normed, egat, me).start()
-
-    def keep_encoded():
-        egat[me] = wide[...].astype(BF16)
-
-    either(p.foreign, swap_encoded, keep_encoded)
-    gs.event(5)
-    pl.when(p.foreign == 1)(swap(1, normed, egat, p.outer).wait_recv)
-    ge.own(1)
-    ge.own(0)
+    ge.event(2)
     load_column.wait()
     repeat(1, PLANE, lambda k: plane_arrival(k).wait_recv())
-    repeat(1, LINE, lambda k: line_copy(k, share).start())
-    gs.event(6)
-
-    def task_table_from(src):
-        def copy():
-            moved = pltpu.make_async_copy(src, task_table, local.at[8])
-            moved.start()
-            moved.wait()
-
-        return copy
-
-    table_copy.wait_recv()
-    either(p.foreign, task_table_from(other_table), task_table_from(table))
+    repeat(1, SIDE, lambda k: line_copy(PAIR * k, share).start())
+    either(p.foreign, task_copies[0].wait, task_copies[1].wait)
+    repeat(0, requests, find_slot)
+    ge.event(3)
     pl.when(p.foreign == 1)(weight_copies[0].wait_recv)
 
     def project(lane, h, dy, db):
@@ -434,96 +469,146 @@
             )
         qs[cut] = acc.astype(BF16)
 
-    ge.event(1)
-    ge.shared(0)
-    visit(UNITS[0] + UNITS[1], UNITS[0], project)
-    ge.event(2)
-    ge.shared(1)
-    visit(UNITS[2], UNITS[1], project)
-    ge.event(3)
-    ge.shared(2)
-    visit(UNITS[3], UNITS[2], project)
+    for event in range(4):
+        ge.shared(event)
+    early_units = UNITS[0] + UNITS[1] + UNITS[2] + UNITS[3]
+    visit(early_units[:5], early_units[:5], project)
+    gs.event(4)
+    visit(early_units[5:], early_units[5:], project)
+    ge.event(4)
+    repeat(0, SIDE, lambda k: line_copy(PAIR * k + 1, share).start())
+    gs.event(5)
+    gs.event(6)
+    gs.event(7)
+    ge.shared(4)
+    visit(UNITS[4], UNITS[4], project)
+    ge.event(5)
     for event in UNITS:
         gs.shared(event)
     pl.when(p.foreign == 1)(weight_copies[1].wait_recv)
-    ge.event(4)
+
+    def sent_states():
+        for h in (0, 1):
+            swap(0, h, qs, sgat, me).wait_send()
+
+    pl.when(p.foreign == 1)(sent_states)
     repeat(0, tokens // 256, query_tile)
-    ge.shared(3)
-    visit(UNITS[4], UNITS[3], project)
-    ge.event(5)
-    ge.shared(4)
-    visit(UNITS[5], UNITS[4], project)
+    ge.shared(5)
     ge.event(6)
-    ge.shared(5)
-    visit(UNITS[6], UNITS[5], project)
+    visit(UNITS[5] + UNITS[6], UNITS[5], project)
+    ge.event(7)
     ge.shared(6)
-    visit([], UNITS[6], project)
-
-    scale = float(HEAD) ** -0.5
-
-    def attend(g):
-        cut = pl.ds(pl.multiple_of(g * GROUP, GROUP), GROUP)
-        one, two = task_table[0, NEIGH * g], task_table[0, NEIGH * g + 1]
-        k = jnp.concatenate([keys[one], keys[two]], axis=0)
-        v = jnp.concatenate([vals[one], vals[two]], axis=0)
-        q = qs[cut]
-        done = []
-        for h in range(width // HEAD):
-            part = slice(h * HEAD, (h + 1) * HEAD)
-            scores = lax.dot_general(
-                q[:, part], k[:, part], (((1,), (1,)), ((), ())), preferred_element_type=F32
-            ) * scale
-            weights = jnp.exp(scores - jnp.max(scores, axis=-1, keepdims=True))
-            probs = weights / jnp.sum(weights, axis=-1, keepdims=True)
-            done.append(jnp.dot(probs.astype(BF16), v[:, part], preferred_element_type=F32))
-        agat[p.mine, cut] = jnp.concatenate(done, axis=1).astype(BF16)
+    visit(UNITS[7], UNITS[6], project)
+    ge.shared(7)
+    visit([], UNITS[7], project)
+
+    power = float(HEAD) ** -0.5 * LOG2E
+
+    def attend(t):
+        scores, held = [], []
+        for g in (2 * t, 2 * t + 1):
+            one, two = slots[NEIGH * g], slots[NEIGH * g + 1]
+            q = qs[pl.ds(pl.multiple_of(g * GROUP, GROUP), GROUP)]
+            k = jnp.concatenate([keys[one], keys[two]], axis=0)
+            held.append(jnp.concatenate([vals[one], vals[two]], axis=0))
+            for h in range(width // HEAD):
+                part = slice(h * HEAD, (h + 1) * HEAD)
+                scores.append(lax.dot_general(
+                    q[:, part], k[:, part], (((1,), (1,)), ((), ())),
+                    preferred_element_type=F32,
+                ))
+        weights = [jnp.exp2((v - jnp.max(v, axis=-1, keepdims=True)) * power) for v in scores]
+        probs = [
+            (w * (1.0 / jnp.sum(w, axis=-1, keepdims=True))).astype(BF16) for w in weights
+        ]
+        heads = width // HEAD
+        rows = []
+        for i in range(2):
+            done = [
+                jnp.dot(
+                    probs[i * heads + h], held[i][:, h * HEAD : (h + 1) * HEAD],
+                    preferred_element_type=F32,
+                )
+                for h in range(heads)
+            ]
+            rows.append(jnp.concatenate(done, axis=1))
+        cut = pl.ds(pl.multiple_of(2 * t * GROUP, 2 * GROUP), 2 * GROUP)
+        agat[p.mine, cut] = jnp.concatenate(rows, axis=0).astype(BF16)
 
     pairs = tokens // GROUP // 2
-    repeat(0, pairs // 2, lambda g: (attend(2 * g), attend(2 * g + 1)))
+    repeat(0, pairs // 2, attend)
     ga.own(0)
-    repeat(pairs // 2, pairs, lambda g: (attend(2 * g), attend(2 * g + 1)))
+    repeat(pairs // 2, pairs, attend)
     ga.own(1)
 
-    repeat(1, LINE, lambda k: line_arrival(k).wait_recv())
     total[...] = jnp.zeros_like(total)
 
     def add_output(lane, h, dy, db):
         j = p.block(lane, dy, db)
-        half = tokens // 2
         cut = pl.ds(pl.multiple_of(h * half, half), half)
         total[cut] += jnp.dot(
             agat[j, cut], wcol[j].reshape(width, width), preferred_element_type=F32
         )
 
-    visit(UNITS[0], [], add_output)
-    for event in range(1, 7):
+    half = tokens // 2
+
+    def swap_out(h):
+        cut = pl.ds(h * half, half)
+        return remote(
+            qs.at[cut], arrived.at[cut], send.at[2, SWAP + h], recv.at[2, SWAP + h], p.partner
+        )
+
+    def finish(h):
+        cut = pl.ds(h * half, half)
+
+        def give():
+            qs[cut] = total[cut].astype(BF16)
+            swap_out(h).start()
+
+        def keep():
+            out[cut] = total[cut].astype(BF16)
+
+        either(p.foreign, give, keep)
+
+    ga.event(1)
+    ga.event(2)
+    repeat(1, LINE, lambda k: line_arrival(k).wait_recv())
+    ga.shared(0)
+    visit(UNITS[0] + UNITS[1], UNITS[0], add_output)
+    for event in (3, 4, 5):
         ga.event(event)
-        ga.shared(event - 1)
-        visit(UNITS[event], UNITS[event - 1], add_output)
+        ga.shared(event - 2)
+        visit(UNITS[event - 1], UNITS[event - 2], add_output)
+    ga.shared(4)
+    visit(UNITS[5], UNITS[4], add_output)
+    ga.shared(5)
+    ga.event(6)
+    visit(UNITS[6], UNITS[5], add_output)
     ga.shared(6)
     visit([], UNITS[6], add_output)
-
-    swap_out = remote(qs, arrived, send.at[2, SWAP], recv.at[2, SWAP], p.partner)
-
-    def swap_output():
-        qs[...] = total[...].astype(BF16)
-        swap_out.start()
-        swap_out.wait_recv()
-        out[...] = arrived[...]
-
-    def keep_output():
-        out[...] = total[...].astype(BF16)
-
-    either(p.foreign, swap_output, keep_output)
+    finish(1)
+    ga.event(7)
+    visit(UNITS[7], [], add_output)
+    ga.shared(7)
+    visit([], UNITS[7], add_output)
+    finish(0)
+
+    def take():
+        for h in (1, 0):
+            cut = pl.ds(h * half, half)
+            swap_out(h).wait_recv()
+            out[cut] = arrived[cut]
+
+    pl.when(p.foreign == 1)(take)
 
     for gather in (gs, ge, ga):
         gather.sent()
     table_copy.wait_send()
 
     def sent_foreign():
-        swap(0, states, sgat, me).wait_send()
-        swap(1, normed, egat, me).wait_send()
-        swap_out.wait_send()
+        for h in (0, 1):
+            swap(1, h, normed, egat, me).wait_send()
+            swap_out(h).wait_send()
 
     def sent_home():
         for copy in weight_copies:
@@ -532,33 +617,22 @@
     either(p.foreign, sent_foreign, sent_home)
     repeat(1, PLANE, lambda k: plane_copy(k).wait_send())
     repeat(1, LINE, lambda k: line_copy(k, share).wait_send())
-
-
-def request_table(requests, own, position):
-    owner = requests // own
-    same = owner[:, None] == owner[None, :]
-    rank = jnp.any(same & (requests[None, :] < requests[:, None]), axis=1)
-    slot = owner * NEIGH + rank.astype(jnp.int32)
-    mine = owner == position
-    low = jnp.min(jnp.where(mine, requests % own, own - 1))
-    high = jnp.max(jnp.where(mine, requests % own, 0))
-    packed = jnp.concatenate([slot, jnp.stack([low, high])]).astype(jnp.int32)
-    return jnp.pad(packed, (0, HEAD - packed.shape[0]))[None, :]
 
 
 def shards(
     decoder_states, w_query, w_key, w_value, w_out, enc_up, enc_down, neighbour_inputs, requests
 ):
     tokens, width = decoder_states.shape
-    own, span, features = neighbour_inputs.shape
-    table = request_table(requests, own, lax.axis_index("an"))
+    _, span, features = neighbour_inputs.shape
     hbm = pl.BlockSpec(memory_space=pl.ANY)
     slots = PLANE * NEIGH
     chunks = enc_up.shape[1] // FCHUNK
     return pl.pallas_call(
         body,
-        out_shape=jax.ShapeDtypeStruct((tokens, width), BF16),
-        in_specs=[pl.BlockSpec(memory_space=pltpu.VMEM)] + [hbm] * 8,
+        out_shape=pltpu.VMEM((tokens, width), BF16),
+        in_specs=[
+            pl.BlockSpec(memory_space=pltpu.SMEM), pl.BlockSpec(memory_space=pltpu.VMEM)
+        ] + [hbm] * 8,
         out_specs=pl.BlockSpec(memory_space=pltpu.VMEM),
         scratch_shapes=[
             pltpu.VMEM((PLANE, tokens, width), BF16),
@@ -578,25 +652,26 @@
             pltpu.VMEM((slots, span, width), BF16),
             pltpu.VMEM((tokens, width), F32),
             pltpu.VMEM((tokens, width), BF16),
-            pltpu.VMEM((1, HEAD), jnp.int32),
-            pltpu.SMEM((1, HEAD), jnp.int32),
-            pltpu.SMEM((1, HEAD), jnp.int32),
-            pltpu.SemaphoreType.DMA((3, SWAP + 1)),
-            pltpu.SemaphoreType.DMA((3, SWAP + 1)),
+            pltpu.VMEM((1, requests.shape[0]), jnp.int32),
+            pltpu.SMEM((1, requests.shape[0]), jnp.int32),
+            pltpu.SMEM(requests.shape, jnp.int32),
+            pltpu.SemaphoreType.DMA((3, SWAP + 2)),
+            pltpu.SemaphoreType.DMA((3, SWAP + 2)),
             pltpu.SemaphoreType.DMA((PLANE,)),
             pltpu.SemaphoreType.DMA((PLANE,)),
             pltpu.SemaphoreType.DMA((LINE,)),
             pltpu.SemaphoreType.DMA((LINE,)),
             pltpu.SemaphoreType.DMA((3,)),
             pltpu.SemaphoreType.DMA((3,)),
-            pltpu.SemaphoreType.DMA((9,)),
+            pltpu.SemaphoreType.DMA((8,)),
             pltpu.SemaphoreType.DMA((2, chunks)),
         ],
         compiler_params=pltpu.CompilerParams(
-            collective_id=0, has_side_effects=True, vmem_limit_bytes=67043328
+            collective_id=0, has_side_effects=True, vmem_limit_bytes=62 * 2**20
         ),
     )(
-        table, decoder_states, w_query, w_key, w_value, w_out, enc_up, enc_down, neighbour_inputs
+        requests, requests[None, :], decoder_states, w_query, w_key, w_value, w_out,
+        enc_up, enc_down, neighbour_inputs,
     )
 
 

time: 147 us -> 119 us (0.81)
  Pallas kernels: 140 us -> 119 us
  other arithmetic: 3.72 us -> 0 us
  local copies, waits for them, and re-layouts: 2.39 us -> 0.8 us
    pallas_call x1, Pallas kernels: 140 us -> 119 us  [shards(): pl.pallas_call(body, out_shape=pltpu.VMEM((tokens, width), BF16), in_spec...]
where the time goes in v3:
time: 119 us
  Pallas kernels  119 us (100%)
    pallas_call x1, Pallas kernels, shards(): pl.pallas_call(body, out_shape=pltpu.VMEM((tokens, width), BF16), in_spec...  119 us

profile of v3, /device:TPU:1, one launch (start us, length us, event | category | flops | bytes accessed | tf_op | source)
XLA Modules:
  0.0 119.3 jit_solution(2634033231418477407)
XLA Ops:
  0.0 118.5 %shard_map.91 = bf16[1024,256]{1,0:T(8,128)(2,1)S(1)} custom-call(s32[32]{0:T(128)} %mine_req.1, s32[1,32]{1,0:T(1,128)} %bitcast.1, bf16[1024,256]{1,0:T(8,128)(2,1)} %states.1, bf16[4096,256]{1,0:T(8,128)(2,1)} %w_query.1, bf16[1024,256]{1,0:T(8,128)(2,1)} %w_key.1, bf16[1024,256]{1,0:T(8,128)(2,1)} %w_value.1, bf16[256,4096]{1,0:T(8,128)(2,1)} %w_out.1, ...), custom_call_target="tpu_custom_call" | custom-call | tf_op jit(solution)/shard_map/pallas_call | solution.py:630
  118.5 0.8 copy.11

commit v4 on v3

--- a/solution.py
+++ b/solution.py
@@ -23,14 +23,18 @@
 
 
 class Gather:
-    def __init__(self, number, buf, send, recv, place):
+    def __init__(self, number, buf, send, recv, place, first=None):
         self.number, self.buf, self.send, self.recv = number, buf, send, recv
         self.place = place
-        self.half = buf.shape[1] // 2
+        first = first or buf.shape[1] // 2
+        self.start = (0, first)
+        self.rows = (first, buf.shape[1] - first)
+
+    def cut(self, h):
+        return pl.ds(self.start[h], self.rows[h])
 
     def copy(self, lane, h, k, dy, db, part, to):
-        rows = self.half
-        first = h * rows
+        rows, first = self.rows[h], self.start[h]
         if part is not None:
             rows = rows // 2
             first += part * rows
@@ -138,10 +142,9 @@
         elif e == 5:
             self.get("a_pair", 3)
             self.get("a_pair", 1)
-        elif e == 6:
-            for i in (0, 1):
-                self.get("b_up2", i)
-                self.get("b_dn2", i)
+        elif e in (6, 7):
+            self.get("b_up2", e - 6)
+            self.get("b_dn2", e - 6)
         else:
             self.get("a_pair", 2)
         self.share(UNITS[e])
@@ -169,8 +172,9 @@
     3: [(0, 2, 0)],
     4: [(1, 3, 1), (1, 1, 1)],
     5: [(0, 3, 1), (0, 1, 1)],
-    6: [(1, 2, 0), (1, 2, 1)],
-    7: [(0, 2, 1)],
+    6: [(1, 2, 0)],
+    7: [(1, 2, 1)],
+    8: [(0, 2, 1)],
 }
 
 
@@ -221,18 +225,22 @@
 
 
 def visit(own, shared, work):
-    units = [(0,) + unit for unit in own] + [(1,) + unit for unit in shared]
-
-    def one(i):
-        picked = []
-        for column in zip(*units):
-            value = jnp.int32(column[0])
-            for k in range(1, len(column)):
-                value = jnp.where(i == k, jnp.int32(column[k]), value)
-            picked.append(value)
-        work(*picked)
-
-    repeat(0, len(units), one)
+    for h in (0, 1):
+        units = [(0,) + unit[1:] for unit in own if unit[0] == h]
+        units += [(1,) + unit[1:] for unit in shared if unit[0] == h]
+
+        def one(i):
+            picked = []
+            for column in zip(*units):
+                value = jnp.int32(column[0])
+                for k in range(1, len(column)):
+                    value = jnp.where(i == k, jnp.int32(column[k]), value)
+                picked.append(value)
+            lane, dy, db = picked
+            work(lane, h, dy, db)
+
+        if units:
+            repeat(0, len(units), one)
 
 
 def body(
@@ -290,21 +298,20 @@
     def greet(to):
         pl.semaphore_signal(barrier, inc=1, device_id=to, device_id_type=pl.DeviceIdType.MESH)
 
-    def line(k):
-        far = k % PAIR
-        at = far * p.outer + (1 - far) * me
-        return {"sa": ((x + k // PAIR) % SIDE) * CORES + p.c, "an": at}
+    def along(dx):
+        return {"sa": ((x + dx) % SIDE) * CORES + p.c, "an": me}
 
     greet(p.partner)
     greet(p.twin)
     repeat(1, PLANE, lambda k: greet({"sa": row, "an": (me + k) % PLANE}))
-    repeat(1, LINE, lambda k: greet(line(k)))
+    greet(along(1))
+    greet(along(3))
 
     load_pool.start()
+    load_rows.start()
     repeat(0, chunks // 2, lambda f: (load_up(f).start(), load_down(f).start()))
     either(p.foreign, stage_states.start, load_states.start)
     repeat(chunks // 2, chunks, lambda f: (load_up(f).start(), load_down(f).start()))
-    load_rows.start()
     load_column.start()
     pl.when(p.foreign == 0)(load_weights)
 
@@ -334,46 +341,18 @@
 
     early = 3
     repeat(0, early, encode_chunk)
-    pl.semaphore_wait(barrier, PLANE - 1 + LINE - 1 + 2)
-
-    gs = Gather(0, sgat, send, recv, p)
+    pl.semaphore_wait(barrier, PLANE - 1 + 4)
+
+    gs = Gather(0, sgat, send, recv, p, first=7 * tokens // 16)
     ge = Gather(1, egat, send, recv, p)
     ga = Gather(2, agat, send, recv, p)
 
-    def swap(number, h, src, buf, to_slot):
-        cut = pl.ds(h * (buf.shape[1] // 2), buf.shape[1] // 2)
+    def swap(gather, h, src, to_slot):
+        cut, number = gather.cut(h), gather.number
         return remote(
-            src.at[cut], buf.at[to_slot, cut],
+            src.at[cut], gather.buf.at[to_slot, cut],
             send.at[number, SWAP + h], recv.at[number, SWAP + h], p.partner,
         )
-
-    def home_states():
-        load_states.wait()
-        gs.own_both()
-
-    def swap_states():
-        stage_states.wait()
-        for h in (0, 1):
-            swap(0, h, qs, sgat, me).start()
-
-    either(p.foreign, swap_states, home_states)
-    table_copy = remote(table, other_table, qsend.at[0], qrecv.at[0], p.twin)
-    table_copy.start()
-    repeat(early, chunks, encode_chunk)
-
-    def swap_encoded():
-        normed[...] = wide[...].astype(BF16)
-        for h in (0, 1):
-            swap(1, h, normed, egat, me).start()
-        for h in (0, 1):
-            swap(0, h, qs, sgat, p.outer).wait_recv()
-            gs.own(h)
-
-    def keep_encoded():
-        egat[me] = wide[...].astype(BF16)
-        ge.own_both()
-
-    either(p.foreign, swap_encoded, keep_encoded)
 
     def plane_copy(k):
         an = (me + k) % PLANE
@@ -390,18 +369,75 @@
             {"sa": row, "an": an},
         )
 
+    def home_states():
+        load_states.wait()
+        gs.own_both()
+
+    def swap_states():
+        stage_states.wait()
+        for h in (0, 1):
+            swap(gs, h, qs, me).start()
+
+    either(p.foreign, swap_states, home_states)
+    load_rows.wait()
+    repeat(1, PLANE, lambda k: plane_copy(k).start())
+    table_copy = remote(table, other_table, qsend.at[0], qrecv.at[0], p.twin)
+    table_copy.start()
+    repeat(early, chunks, encode_chunk)
+
     def plane_arrival(k):
         ref = wcol.at[(me + PLANE - k) % PLANE, share]
         return remote(ref, ref, wsend.at[k], wrecv.at[k], {"sa": row, "an": (me + k) % PLANE})
 
-    def line_copy(k, held):
+    def across(held):
         ref = wcol.at[:, held]
-        return remote(ref, ref, lsend.at[k], lrecv.at[k], line(k))
-
-    def line_arrival(k):
-        far = k % PAIR
-        part = b + far * (1 - 2 * b)
-        return line_copy(k, ((x + SIDE - k // PAIR) % SIDE) * PAIR + part)
+        return remote(ref, ref, lsend.at[0], lrecv.at[0], p.holder)
+
+    def along_copy(k, held, to, part=None):
+        blocks = pl.ds(0, PLANE) if part is None else pl.ds(part * (PLANE // 2), PLANE // 2)
+        ref = wcol.at[blocks, pl.ds((held % SIDE) * PAIR, PAIR)]
+        return remote(ref, ref, lsend.at[k], lrecv.at[k], along(to))
+
+    def spread1():
+        load_column.wait()
+        repeat(1, PLANE, lambda k: plane_arrival(k).wait_recv())
+        across(share).start()
+
+    def spread2():
+        across(share + 1 - 2 * b).wait_recv()
+        along_copy(1, x, 1).start()
+        along_copy(2, x, 3).start()
+
+    def spread3():
+        along_copy(1, x + 3, 1).wait_recv()
+        along_copy(3, x + 3, 1, 0).start()
+        along_copy(2, x + 1, 3).wait_recv()
+        along_copy(4, x + 1, 3, 1).start()
+
+    def spread4():
+        along_copy(3, x + 2, 1, 0).wait_recv()
+        along_copy(4, x + 2, 3, 1).wait_recv()
+
+    def spread_sent():
+        across(share).wait_send()
+        along_copy(1, x, 1).wait_send()
+        along_copy(2, x, 3).wait_send()
+        along_copy(3, x, 1, 0).wait_send()
+        along_copy(4, x, 3, 1).wait_send()
+
+    def swap_encoded():
+        normed[...] = wide[...].astype(BF16)
+        for h in (0, 1):
+            swap(ge, h, normed, me).start()
+        for h in (0, 1):
+            swap(gs, h, qs, p.outer).wait_recv()
+            gs.own(h)
+
+    def keep_encoded():
+        egat[me] = wide[...].astype(BF16)
+        ge.own_both()
+
+    either(p.foreign, swap_encoded, keep_encoded)
 
     weight_copies = (
         remote(wkv, wkv, qsend.at[1], qrecv.at[1], p.holder),
@@ -417,13 +453,12 @@
 
     def late_encoded():
         for h in (0, 1):
-            swap(1, h, normed, egat, p.outer).wait_recv()
+            swap(ge, h, normed, p.outer).wait_recv()
             ge.own(h)
+        spread1()
 
     pl.when(p.foreign == 1)(late_encoded)
     gs.event(1)
-    load_rows.wait()
-    repeat(1, PLANE, lambda k: plane_copy(k).start())
     table_copy.wait_recv()
     task_copies = [
         pltpu.make_async_copy(src, task_req, local.at[7]) for src in (other_table, table)
@@ -439,19 +474,6 @@
             later = jnp.where((other < wanted) & (other >= owner * own), jnp.int32(1), later)
         slots[k] = owner * NEIGH + later
 
-    gs.event(2)
-    pl.when(p.foreign == 0)(give_weights)
-    ge.event(1)
-    gs.event(3)
-    ge.event(2)
-    load_column.wait()
-    repeat(1, PLANE, lambda k: plane_arrival(k).wait_recv())
-    repeat(1, SIDE, lambda k: line_copy(PAIR * k, share).start())
-    either(p.foreign, task_copies[0].wait, task_copies[1].wait)
-    repeat(0, requests, find_slot)
-    ge.event(3)
-    pl.when(p.foreign == 1)(weight_copies[0].wait_recv)
-
     def project(lane, h, dy, db):
         block = p.block(lane, dy, db)
         slot = block * NEIGH + h
@@ -460,47 +482,85 @@
         keys[slot] = both[:, :width].astype(BF16)
         vals[slot] = both[:, width:].astype(BF16)
 
-    def query_tile(t):
-        cut = pl.ds(pl.multiple_of(t * 256, 256), 256)
-        acc = jnp.zeros((256, width), F32)
-        for j in range(PLANE):
-            acc = acc + jnp.dot(
-                sgat[j, cut], wq[j * width : (j + 1) * width], preferred_element_type=F32
-            )
-        qs[cut] = acc.astype(BF16)
-
-    for event in range(4):
+    query_early = [u for e in range(5) for u in UNITS[e]]
+    query_late = [u for e in range(5, 9) for u in UNITS[e]]
+
+    def query_part(units, last):
+        for h in (0, 1):
+            blocks = [(lane, dy, db) for lane in (0, 1) for (k, dy, db) in units if k == h]
+            rows = gs.rows[h] // 2
+
+            def tile(t):
+                cut = pl.ds(pl.multiple_of(gs.start[h] + t * rows, 32), rows)
+                acc = total[cut] if last else jnp.zeros((rows, width), F32)
+                for at in blocks:
+                    j = p.block(*at)
+                    acc = acc + jnp.dot(
+                        sgat[j, cut], wq[pl.ds(pl.multiple_of(j * width, width), width)],
+                        preferred_element_type=F32,
+                    )
+                if last:
+                    qs[cut] = acc.astype(BF16)
+                else:
+                    total[cut] = acc
+
+            repeat(0, 2, tile)
+
+    gs.event(2)
+    def spread1_then_weights():
+        spread1()
+        give_weights()
+
+    either(p.foreign, spread2, spread1_then_weights)
+    ge.event(1)
+    gs.event(3)
+    pl.when(p.foreign == 0)(spread2)
+    ge.event(2)
+    either(p.foreign, task_copies[0].wait, task_copies[1].wait)
+    repeat(0, requests, find_slot)
+    pl.when(p.foreign == 1)(weight_copies[0].wait_recv)
+    visit(UNITS[0] + UNITS[1], [], project)
+    ge.event(3)
+    spread3()
+    visit(UNITS[2] + UNITS[3], [], project)
+    gs.event(4)
+    for event in (0, 1):
         ge.shared(event)
-    early_units = UNITS[0] + UNITS[1] + UNITS[2] + UNITS[3]
-    visit(early_units[:5], early_units[:5], project)
-    gs.event(4)
-    visit(early_units[5:], early_units[5:], project)
+    visit([], UNITS[0] + UNITS[1], project)
     ge.event(4)
-    repeat(0, SIDE, lambda k: line_copy(PAIR * k + 1, share).start())
-    gs.event(5)
-    gs.event(6)
-    gs.event(7)
-    ge.shared(4)
-    visit(UNITS[4], UNITS[4], project)
-    ge.event(5)
-    for event in UNITS:
+    for event in (2, 3):
+        ge.shared(event)
+    visit(UNITS[4], UNITS[2] + UNITS[3], project)
+    for event in range(5):
         gs.shared(event)
-    pl.when(p.foreign == 1)(weight_copies[1].wait_recv)
 
     def sent_states():
         for h in (0, 1):
-            swap(0, h, qs, sgat, me).wait_send()
-
-    pl.when(p.foreign == 1)(sent_states)
-    repeat(0, tokens // 256, query_tile)
+            swap(gs, h, qs, me).wait_send()
+
+    def foreign_ready():
+        weight_copies[1].wait_recv()
+        sent_states()
+
+    pl.when(p.foreign == 1)(foreign_ready)
+    gs.event(5)
+    query_part(query_early, False)
+    for event in (6, 7, 8):
+        gs.event(event)
+    ge.event(5)
+    ge.shared(4)
+    visit(UNITS[5], UNITS[4], project)
+    for event in (5, 6, 7, 8):
+        gs.shared(event)
+    for event in (6, 7, 8):
+        ge.event(event)
+    query_part(query_late, True)
     ge.shared(5)
-    ge.event(6)
-    visit(UNITS[5] + UNITS[6], UNITS[5], project)
-    ge.event(7)
     ge.shared(6)
-    visit(UNITS[7], UNITS[6], project)
+    visit(UNITS[6] + UNITS[7] + UNITS[8], UNITS[5] + UNITS[6], project)
     ge.shared(7)
-    visit([], UNITS[7], project)
+    ge.shared(8)
+    visit([], UNITS[7] + UNITS[8], project)
 
     power = float(HEAD) ** -0.5 * LOG2E
 
@@ -572,25 +632,30 @@
 
     ga.event(1)
     ga.event(2)
-    repeat(1, LINE, lambda k: line_arrival(k).wait_recv())
+    spread4()
     ga.shared(0)
     visit(UNITS[0] + UNITS[1], UNITS[0], add_output)
-    for event in (3, 4, 5):
+    for event in (3, 4):
         ga.event(event)
         ga.shared(event - 2)
         visit(UNITS[event - 1], UNITS[event - 2], add_output)
+    ga.shared(3)
+    visit(UNITS[4], UNITS[3], add_output)
+    ga.event(5)
+    ga.event(6)
     ga.shared(4)
-    visit(UNITS[5], UNITS[4], add_output)
+    visit(UNITS[5] + UNITS[6], UNITS[4], add_output)
+    ga.event(7)
     ga.shared(5)
-    ga.event(6)
-    visit(UNITS[6], UNITS[5], add_output)
     ga.shared(6)
-    visit([], UNITS[6], add_output)
-    finish(1)
-    ga.event(7)
-    visit(UNITS[7], [], add_output)
+    visit(UNITS[7], UNITS[5] + UNITS[6], add_output)
     ga.shared(7)
     visit([], UNITS[7], add_output)
+    finish(1)
+    ga.event(8)
+    visit(UNITS[8], [], add_output)
+    ga.shared(8)
+    visit([], UNITS[8], add_output)
     finish(0)
 
     def take():
@@ -607,7 +672,7 @@
 
     def sent_foreign():
         for h in (0, 1):
-            swap(1, h, normed, egat, me).wait_send()
+            swap(ge, h, normed, me).wait_send()
             swap_out(h).wait_send()
 
     def sent_home():
@@ -616,7 +681,7 @@
 
     either(p.foreign, sent_foreign, sent_home)
     repeat(1, PLANE, lambda k: plane_copy(k).wait_send())
-    repeat(1, LINE, lambda k: line_copy(k, share).wait_send())
+    spread_sent()
 
 
 def shards(
@@ -659,8 +724,8 @@
             pltpu.SemaphoreType.DMA((3, SWAP + 2)),
             pltpu.SemaphoreType.DMA((PLANE,)),
             pltpu.SemaphoreType.DMA((PLANE,)),
-            pltpu.SemaphoreType.DMA((LINE,)),
-            pltpu.SemaphoreType.DMA((LINE,)),
+            pltpu.SemaphoreType.DMA((5,)),
+            pltpu.SemaphoreType.DMA((5,)),
             pltpu.SemaphoreType.DMA((3,)),
             pltpu.SemaphoreType.DMA((3,)),
             pltpu.SemaphoreType.DMA((8,)),

time: 119 us -> 116 us (0.975)
  Pallas kernels: 119 us -> 115 us
    pallas_call x1, Pallas kernels: 119 us -> 115 us  [shards(): pl.pallas_call(body, out_shape=pltpu.VMEM((tokens, width), BF16), in_spec...]
where the time goes in v4:
time: 116 us
  Pallas kernels  115 us (99%)
    pallas_call x1, Pallas kernels, shards(): pl.pallas_call(body, out_shape=pltpu.VMEM((tokens, width), BF16), in_spec...  115 us

profile of v4, /device:TPU:1, one launch (start us, length us, event | category | flops | bytes accessed | tf_op | source)
XLA Modules:
  0.0 115.8 jit_solution(4505663781848044457)
XLA Ops:
  0.0 115.0 %shard_map.91 = bf16[1024,256]{1,0:T(8,128)(2,1)S(1)} custom-call(s32[32]{0:T(128)} %mine_req.1, s32[1,32]{1,0:T(1,128)} %bitcast.1, bf16[1024,256]{1,0:T(8,128)(2,1)} %states.1, bf16[4096,256]{1,0:T(8,128)(2,1)} %w_query.1, bf16[1024,256]{1,0:T(8,128)(2,1)} %w_key.1, bf16[1024,256]{1,0:T(8,128)(2,1)} %w_value.1, bf16[256,4096]{1,0:T(8,128)(2,1)} %w_out.1, ...), custom_call_target="tpu_custom_call" | custom-call | tf_op jit(solution)/shard_map/pallas_call | solution.py:695
  115.0 0.8 copy.11

commit v5 on v4

--- a/solution.py
+++ b/solution.py
@@ -42,7 +42,7 @@
         return pltpu.make_async_remote_copy(
             src_ref=ref,
             dst_ref=ref,
-            send_sem=self.send.at[self.number, k],
+            send_sem=self.send.at[self.number],
             recv_sem=self.recv.at[self.number, k],
             device_id=to,
             device_id_type=pl.DeviceIdType.MESH,
@@ -150,19 +150,14 @@
         self.share(UNITS[e])
 
     def sent(self):
-        for name, count in MESSAGES:
-            for i in range(count):
-                h, k, sent, _, part, to = self.message(name, i)
-                self.copy(0, h, k, *sent, part, to).wait_send()
-        for event in UNITS:
-            for unit in UNITS[event]:
-                self.across(0, unit).wait_send()
-
-
-MESSAGES = (
-    ("a_up", 1), ("a_dn", 1), ("a_up2", 1), ("a_dn2", 1), ("a_pair", 4),
-    ("b_pair", 1), ("b_up", 2), ("b_dn", 2), ("b_up2", 2), ("b_dn2", 2),
-)
+        ref = self.buf.at[pl.ds(0, PLANE - 1)]
+        pltpu.make_async_remote_copy(
+            src_ref=ref, dst_ref=ref, send_sem=self.send.at[self.number],
+            recv_sem=self.recv.at[self.number, 0], device_id=self.place.pair,
+            device_id_type=pl.DeviceIdType.MESH,
+        ).wait_send()
+
+
 ROUTED = 17
 SWAP = 33
 UNITS = {
@@ -247,7 +242,7 @@
     mine_req, table, states, w_query, w_key, w_value, w_out, enc_up, enc_down, nearby, out,
     sgat, egat, agat, wcol, wq, wkv, wrow, up, down, pool,
     wide, normed, qs, keys, vals, total, arrived, other_table, task_req, slots,
-    send, recv, wsend, wrecv, lsend, lrecv, qsend, qrecv, local, wsem,
+    send, swapped, recv, wsend, wrecv, lsend, lrecv, qsend, qrecv, local, wsem,
 ):
     p = Place()
     row, me, x, b = p.row, p.me, p.x, p.b
@@ -351,7 +346,7 @@
         cut, number = gather.cut(h), gather.number
         return remote(
             src.at[cut], gather.buf.at[to_slot, cut],
-            send.at[number, SWAP + h], recv.at[number, SWAP + h], p.partner,
+            swapped.at[number, h], recv.at[number, SWAP + h], p.partner,
         )
 
     def plane_copy(k):
@@ -364,8 +359,8 @@
                 pl.ds(pl.multiple_of(task * width, width), width),
             ],
             wcol.at[me, x * PAIR + part],
-            wsend.at[k],
-            wrecv.at[k],
+            wsend.at[0],
+            wrecv.at[0],
             {"sa": row, "an": an},
         )
 
@@ -385,9 +380,9 @@
     table_copy.start()
     repeat(early, chunks, encode_chunk)
 
-    def plane_arrival(k):
-        ref = wcol.at[(me + PLANE - k) % PLANE, share]
-        return remote(ref, ref, wsend.at[k], wrecv.at[k], {"sa": row, "an": (me + k) % PLANE})
+    def plane_all():
+        ref = wcol.at[pl.ds(0, PLANE - 1), share]
+        return remote(ref, ref, wsend.at[0], wrecv.at[0], p.pair)
 
     def across(held):
         ref = wcol.at[:, held]
@@ -400,7 +395,7 @@
 
     def spread1():
         load_column.wait()
-        repeat(1, PLANE, lambda k: plane_arrival(k).wait_recv())
+        plane_all().wait_recv()
         across(share).start()
 
     def spread2():
@@ -542,8 +537,8 @@
         weight_copies[1].wait_recv()
         sent_states()
 
+    gs.event(5)
     pl.when(p.foreign == 1)(foreign_ready)
-    gs.event(5)
     query_part(query_early, False)
     for event in (6, 7, 8):
         gs.event(event)
@@ -615,7 +610,7 @@
     def swap_out(h):
         cut = pl.ds(h * half, half)
         return remote(
-            qs.at[cut], arrived.at[cut], send.at[2, SWAP + h], recv.at[2, SWAP + h], p.partner
+            qs.at[cut], arrived.at[cut], swapped.at[2, h], recv.at[2, SWAP + h], p.partner
         )
 
     def finish(h):
@@ -680,7 +675,7 @@
             copy.wait_send()
 
     either(p.foreign, sent_foreign, sent_home)
-    repeat(1, PLANE, lambda k: plane_copy(k).wait_send())
+    plane_all().wait_send()
     spread_sent()
 
 
@@ -720,10 +715,11 @@
             pltpu.VMEM((1, requests.shape[0]), jnp.int32),
             pltpu.SMEM((1, requests.shape[0]), jnp.int32),
             pltpu.SMEM(requests.shape, jnp.int32),
+            pltpu.SemaphoreType.DMA((3,)),
+            pltpu.SemaphoreType.DMA((3, 2)),
             pltpu.SemaphoreType.DMA((3, SWAP + 2)),
-            pltpu.SemaphoreType.DMA((3, SWAP + 2)),
-            pltpu.SemaphoreType.DMA((PLANE,)),
-            pltpu.SemaphoreType.DMA((PLANE,)),
+            pltpu.SemaphoreType.DMA((1,)),
+            pltpu.SemaphoreType.DMA((1,)),
             pltpu.SemaphoreType.DMA((5,)),
             pltpu.SemaphoreType.DMA((5,)),
             pltpu.SemaphoreType.DMA((3,)),

time: 116 us -> 115 us (level)
    pallas_call x1, Pallas kernels: 115 us -> 114 us  [shards(): pl.pallas_call(body, out_shape=pltpu.VMEM((tokens, width), BF16), in_spec...]
where the time goes in v5:
time: 115 us
  Pallas kernels  114 us (99%)
    pallas_call x1, Pallas kernels, shards(): pl.pallas_call(body, out_shape=pltpu.VMEM((tokens, width), BF16), in_spec...  114 us

profile of v5, /device:TPU:1, one launch (start us, length us, event | category | flops | bytes accessed | tf_op | source)
XLA Modules:
  0.0 114.6 jit_solution(5650976147052337092)
XLA Ops:
  0.0 113.8 %shard_map.91 = bf16[1024,256]{1,0:T(8,128)(2,1)S(1)} custom-call(s32[32]{0:T(128)} %mine_req.1, s32[1,32]{1,0:T(1,128)} %bitcast.1, bf16[1024,256]{1,0:T(8,128)(2,1)} %states.1, bf16[4096,256]{1,0:T(8,128)(2,1)} %w_query.1, bf16[1024,256]{1,0:T(8,128)(2,1)} %w_key.1, bf16[1024,256]{1,0:T(8,128)(2,1)} %w_value.1, bf16[256,4096]{1,0:T(8,128)(2,1)} %w_out.1, ...), custom_call_target="tpu_custom_call" | custom-call | tf_op jit(solution)/shard_map/pallas_call | solution.py:690
  113.8 0.8 copy.11

commit v6 on v5

--- a/solution.py
+++ b/solution.py
@@ -538,13 +538,14 @@
         sent_states()
 
     gs.event(5)
+    ge.shared(4)
+    visit([], UNITS[4], project)
     pl.when(p.foreign == 1)(foreign_ready)
     query_part(query_early, False)
     for event in (6, 7, 8):
         gs.event(event)
     ge.event(5)
-    ge.shared(4)
-    visit(UNITS[5], UNITS[4], project)
+    visit(UNITS[5], [], project)
     for event in (5, 6, 7, 8):
         gs.shared(event)
     for event in (6, 7, 8):

time: 115 us -> 115 us (level)
  no operation moved by 1% of the time
where the time goes in v6:
time: 115 us
  Pallas kernels  114 us (99%)
    pallas_call x1, Pallas kernels, shards(): pl.pallas_call(body, out_shape=pltpu.VMEM((tokens, width), BF16), in_spec...  114 us

profile of v6, /device:TPU:1, one launch (start us, length us, event | category | flops | bytes accessed | tf_op | source)
XLA Modules:
  0.0 114.6 jit_solution(14877509984660294164)
XLA Ops:
  0.0 113.8 %shard_map.91 = bf16[1024,256]{1,0:T(8,128)(2,1)S(1)} custom-call(s32[32]{0:T(128)} %mine_req.1, s32[1,32]{1,0:T(1,128)} %bitcast.1, bf16[1024,256]{1,0:T(8,128)(2,1)} %states.1, bf16[4096,256]{1,0:T(8,128)(2,1)} %w_query.1, bf16[1024,256]{1,0:T(8,128)(2,1)} %w_key.1, bf16[1024,256]{1,0:T(8,128)(2,1)} %w_value.1, bf16[256,4096]{1,0:T(8,128)(2,1)} %w_out.1, ...), custom_call_target="tpu_custom_call" | custom-call | tf_op jit(solution)/shard_map/pallas_call | solution.py:691
  113.8 0.8 copy.11
